TPU v7x, 256 devices: a whole 4x4x8 slice. The times are simulated.
256 devices in a mesh: dp: 16 (over y, x), mp: 16 (over z, core).
Axes of the slice: x: 4, y: 4, z: 8, core: 2. Of those that a mesh axis runs over, the one named last changes fastest.
Arguments:
- data_rows: bfloat16 [131072, 2048], P(('dp', 'mp')), may hold values from -32 to 32
- centroids: bfloat16 [12288, 2048], P('mp'), may hold values from -0.75 to 0.75
- block_mask: int32 [16, 1024], P(None, ('dp', 'mp')), may hold values from 0 to 1, as said below
- lower_bound: float32 [16, 131072], P(None, ('dp', 'mp')), may hold values from 0 to 4
Outputs:
- new_centroids: float32 [12288, 2048], P(('mp', 'dp'))
- centroid_shift: float32 [12288], P(('mp', 'dp'))
- log_norm: float32 [131072], P(('dp', 'mp'))
- new_lower: float32 [16, 131072], P(None, ('dp', 'mp'))
Inputs may be any that keep to these rules, and one draw needn't show every extreme that they name: `block_mask`: within the 4 blocks of one device (aligned runs along the last dimension), at most 1 are 1 for each shard; for some shard every device has exactly 1.
All inputs are finite; a program needn't handle non-finite values.
Results may differ from a plain program's by a relative error of at most 0.0011.
Values may be sent and summed in bfloat16 or wider, within the bound.
A program may use at most 128 MiB of HBM per device.

v0:
```python
import math

import jax
import jax.numpy as jnp
from jax import lax
from jax.sharding import Mesh
from jax.sharding import PartitionSpec as P

BLOCK = 128
SLOTS = 1
MP = ("mp_0", "mp_1")
DP_MP = ("dp", "mp_0", "mp_1")
MP_DP = ("mp_0", "mp_1", "dp")


def gathered_once(array, axis):
    leaves = jax.tree.leaves(array)
    order = sorted(range(len(leaves)), key=lambda k: -leaves[k].size)
    width = (1, *leaves[order[0]].shape)[-1]
    lines = [
        jnp.pad(leaves[k].reshape(-1), (0, -leaves[k].size % width)).reshape(-1, width)
        for k in order
    ]
    both, at, found = (lax.all_gather(jnp.concatenate(lines), axis), 0, {})
    for k, line in zip(order, lines):
        piece = both[:, at : at + len(line)].reshape(len(both), -1)
        found[k] = piece[:, : leaves[k].size].reshape(-1, *leaves[k].shape)
        at += len(line)
    numbers = iter(range(len(leaves)))
    return jax.tree.map(lambda _: found[next(numbers)], array)


def joined_all(array, axes, combine):
    for axis in axes:
        pieces = gathered_once(array, axis)
        array = jax.tree.map(lambda part: part[0], pieces)
        for k in range(1, lax.axis_size(axis)):
            array = combine(array, jax.tree.map(lambda part: part[k], pieces))
    return array


def pack_codes(mask_dev, slot_total):
    block_count = mask_dev.shape[1]
    block_rank = jnp.cumsum(mask_dev, axis=1) - 1
    slot_ids = jnp.arange(slot_total, dtype=jnp.int32)
    chosen = (mask_dev[:, None, :] == 1) & (block_rank[:, None, :] == slot_ids[None, :, None])
    labels = jnp.arange(1, block_count + 1, dtype=jnp.int32)
    return jnp.sum(jnp.where(chosen, labels[None, None, :], 0), axis=2)


def slot_marks(slot_codes, block_count):
    labels = jnp.arange(1, block_count + 1, dtype=jnp.int32)
    return slot_codes[:, :, None] == labels[None, None, :]


def softmax_pair(first, second):
    best = jnp.maximum(first[0], second[0])
    return (best, first[1] * jnp.exp(first[0] - best) + second[1] * jnp.exp(second[0] - best))


def on_device(data_rows, centroids, block_mask, lower_bound):
    feat = data_rows.shape[1]
    block_count = data_rows.shape[0] // BLOCK
    shard_count = lax.axis_size(MP)
    sharpness = 4.0 / math.sqrt(feat)
    slot_codes = pack_codes(block_mask, SLOTS)
    row_blocks = data_rows.reshape(block_count, BLOCK, feat)
    outgoing = jnp.take(row_blocks, jnp.maximum(slot_codes - 1, 0), axis=0)
    outgoing = jnp.where((slot_codes > 0)[:, :, None, None], outgoing, jnp.zeros_like(outgoing))
    cent_norm = jnp.sum(jnp.square(centroids.astype(jnp.float32)), axis=1)
    piece_rows = lax.all_to_all(outgoing, MP, split_axis=0, concat_axis=0, tiled=True)
    piece_codes = lax.all_to_all(
        slot_codes.astype(jnp.bfloat16), MP, split_axis=0, concat_axis=0, tiled=True
    )
    products = jnp.einsum(
        "sbif,kf->sbik", piece_rows, centroids, preferred_element_type=jnp.float32
    )
    scores = sharpness * (2.0 * products - cent_norm)
    is_valid = (piece_codes > 0)[:, :, None]
    best = jnp.max(scores, axis=3)
    row_top = jnp.where(is_valid, best, -1e30)
    row_mass = jnp.where(is_valid, jnp.sum(jnp.exp(scores - best[..., None]), axis=3), 0.0)
    got_rows, got_codes, scores, row_top, row_mass = (
        piece_rows,
        piece_codes,
        scores,
        row_top,
        row_mass,
    )
    is_slot = slot_marks(got_codes.astype(jnp.int32), block_count)
    group_top = jnp.max(jnp.where(is_slot[..., None], row_top[:, :, None, :], -1e30), axis=1)
    spread = row_mass[:, :, None, :] * jnp.exp(row_top[:, :, None, :] - group_top[:, None])
    group_mass = jnp.sum(jnp.where(is_slot[..., None], spread, 0.0), axis=1)
    all_top, all_mass = joined_all((group_top, group_mass), MP, softmax_pair)
    ceiling = jnp.maximum(all_top, 0.0)
    row_norm = ceiling + jnp.log(jnp.exp(-ceiling) + all_mass * jnp.exp(all_top - ceiling))
    slot_norm = jnp.sum(jnp.where(is_slot[..., None], row_norm[:, None], 0.0), axis=2)
    own_norm = lax.dynamic_index_in_dim(row_norm, lax.axis_index(MP), 0, keepdims=False)
    log_norm = own_norm.reshape(-1)
    is_valid = (got_codes > 0)[:, :, None, None]
    weight = jnp.where(is_valid, jnp.exp(scores - slot_norm[..., None]), 0.0)
    counts = jnp.sum(weight, axis=(0, 1, 2))
    weight_half = weight.astype(jnp.bfloat16)
    weighted = jnp.einsum(
        "sbik,sbif->kf", weight_half, got_rows, preferred_element_type=jnp.float32
    )
    part_sums, part_counts = (
        lax.psum_scatter(weighted, "dp", scatter_dimension=0, tiled=True),
        lax.psum_scatter(counts, "dp", scatter_dimension=0, tiled=True),
    )
    own_width = part_sums.shape[0]
    old_cents = lax.dynamic_slice_in_dim(
        centroids, lax.axis_index("dp") * own_width, own_width, 0
    ).astype(jnp.float32)
    updated = (part_sums + old_cents) / (part_counts[:, None] + 1.0)
    movement = jnp.sqrt(jnp.sum(jnp.square(updated - old_cents), axis=1) + 1.0)
    shard_peaks = lax.all_gather(jnp.max(movement)[None], DP_MP, axis=0, tiled=True)
    shard_peak = jnp.max(shard_peaks.reshape(-1, shard_count), axis=0)
    new_lower = lower_bound - shard_peak[:, None]
    return (updated, movement, log_norm, new_lower)


def solution(mesh):
    torus = Mesh(mesh.devices.reshape(mesh.shape["dp"], 8, 2), ("dp", "mp_0", "mp_1"))
    in_specs = (P(DP_MP, None), P(MP, None), P(None, DP_MP), P(None, DP_MP))
    out_specs = (P(MP_DP, None), P(MP_DP), P(DP_MP), P(None, DP_MP))
    return jax.shard_map(
        on_device, mesh=torus, in_specs=in_specs, out_specs=out_specs, check_vma=False
    )
```

profile of v0, /device:TPU:1, one launch (start us, length us, event | category | flops | bytes accessed | tf_op | source)
XLA Modules:
  0.0 447.8 jit_solution(5318225488769490541)
XLA Ops:
  7.2 0.9 reduce_window_sum.11
  8.0 0.8 select_reduce_fusion.1
  8.8 0.7 copy.20
  9.5 10.0 %all-to-all-start = ((bf16[16,1,1]{2,1,0:T(2,128)(2,1)}), bf16[16,1,1]{2,1,0:T(2,128)(2,1)S(1)}, u32[]{:S(2)}, u32[]{:S(2)}) async-start(bf16[16,1,1]{2,1,0:T(2,128)(2,1)} %copy.20), calls=%async_computation | async-start | bytes 16384 | tf_op jit(solution)/shard_map/all_to_all | solution.py:72
  19.5 4.7 %gather_fusion = bf16[16,128,2048]{2,1,0:T(8,128)(2,1)} fusion(bf16[4,128,2048]{2,1,0:T(8,128)(2,1)S(1)} %bitcast.206, s32[1024]{0:T(1024)S(1)} %pad_clamp_fusion), kind=kCustom, calls=%fused_computation | custom fusion | bytes 16777280 | tf_op jit(solution)/shard_map/jit(_take)/gather | solution.py:68
  24.2 7.6 %fusion.4 = bf16[16,1,128,2048]{3,2,1,0:T(8,128)(2,1)} fusion(bf16[16,128,2048]{2,1,0:T(8,128)(2,1)} %gather_fusion, pred[16]{0:T(512)(128)(4,1)S(1)} %get-tuple-element.25, pred[16]{0:T(512)(128)(4,1)S(1)} %get-tuple-element.24), kind=kLoop, calls=%fused_computation.6 | loop fusion | flops 8388608 | bytes 16777248 | tf_op jit(solution)/shard_map/jit(_where)/select_n | solution.py:69
  31.8 7.1 %all-to-all-start.1 = ((bf16[16,1,128,2048]{3,2,1,0:T(8,128)(2,1)}), bf16[16,1,128,2048]{3,2,1,0:T(8,128)(2,1)}, u32[]{:S(2)}, u32[]{:S(2)}) async-start(bf16[16,1,128,2048]{3,2,1,0:T(8,128)(2,1)} %fusion.4), calls=%async_computation.1 | async-start | bytes 16777216 | tf_op jit(solution)/shard_map/all_to_all | solution.py:71
  39.1 2.6 multiply_reduce_fusion
  42.8 179.6 %all-to-all-done.1 = bf16[16,1,128,2048]{3,2,1,0:T(8,128)(2,1)} async-done(((bf16[16,1,128,2048]{3,2,1,0:T(8,128)(2,1)}), bf16[16,1,128,2048]{3,2,1,0:T(8,128)(2,1)}, u32[]{:S(2)}, u32[]{:S(2)}) %all-to-all-start.1) | async-done | bytes 8388640 | tf_op jit(solution)/shard_map/all_to_all | solution.py:71
  222.3 10.5 %fusion.15 = (f32[16,128]{1,0:T(8,128)S(1)}, f32[16,128,768]{2,1,0:T(8,128)S(1)}) fusion(f32[768]{0:T(1024)S(1)} %multiply_reduce_fusion, bf16[768,2048]{1,0:T(8,128)(2,1)} %param.5, bf16[16,1,128,2048]{3,2,1,0:T(8,128)(2,1)} %all-to-all-done.1), kind=kOutput, calls=%fused_computation.18 | convolution fusion | flops 6448740352 | bytes 17837056 | tf_op jit(solution)/shard_map/sbif,kf->sbik/dot_general | solution.py:75
  232.8 1.7 exponential_reduce_fusion
  234.8 19.7 %all-gather = f32[1024,128]{1,0:T(8,128)S(1)} all-gather(f32[128,128]{1,0:T(8,128)S(1)} %pad_maximum_fusion), channel_id=2, replica_groups=mesh['dp'=16,'mp_0'=8,'mp_1'=2] {'mp_0'}, dimensions={0}, use_global_device_ids=true | all-gather | bytes 589824 | tf_op jit(solution)/shard_map/all_gather | solution.py:24
  254.6 8.6 %all-gather.1 = f32[256,128]{1,0:T(8,128)S(1)} all-gather(f32[128,128]{1,0:T(8,128)S(1)} %pad_maximum_fusion.1), channel_id=3, replica_groups=mesh['dp'=16,'mp_0'=8,'mp_1'=2] {'mp_1'}, dimensions={0}, use_global_device_ids=true | all-gather | bytes 196608 | tf_op jit(solution)/shard_map/all_gather | solution.py:24
  263.3 11.8 %fusion.7 = f32[768,2048]{1,0:T(8,128)} fusion(bf16[16,1,128,2048]{3,2,1,0:T(8,128)(2,1)} %all-to-all-done.1, f32[16,128]{1,0:T(8,128)S(1)} %select_reduce_fusion, pred[16]{0:T(512)(128)(4,1)S(1)} %compare_reduce_fusion, f32[16,128,768]{2,1,0:T(8,128)S(1)} %get-tuple-element.27, f32[768]{0:T(1024)S(1)} %multiply_reduce_fusion), kind=kOutput, calls=%fused_computation.13 | convolution fusion | flops 6451888128 | bytes 20982800 | tf_op jit(solution)/shard_map/sbik,sbif->kf/dot_general | solution.py:104
  275.2 0.6 copy-done.3
  277.1 3.7 fusion.5
  280.8 33.8 %all-reduce.1 = f32[768]{0:T(1024)S(1)} all-reduce(f32[768]{0:T(1024)S(1)} %fusion.5), channel_id=5, replica_groups=mesh['dp'=16,'mp_0'=8,'mp_1'=2] {'dp'}, use_global_device_ids=true, to_apply=%region_8.9.clone | all-reduce | flops 768 | bytes 6144
  314.7 0.6 fusion.59
  315.3 43.5 %reduce-scatter.2.cloned.1.call-done = f32[48,2048]{1,0:T(8,128)} async-done(((f32[768,2048]{1,0:T(8,128)}), f32[48,2048]{1,0:T(8,128)}) %reduce-scatter.2.cloned.1.call-update) | async-done | bytes 393232 | tf_op jit(solution)/shard_map/reduce_scatter | solution.py:108
  358.9 2.1 fusion.18
  361.0 1.1 fusion.65
  362.1 0.8 dynamic-update-slice
  362.9 77.2 %all-reduce = f32[256]{0:T(256)S(1)} all-reduce(f32[256]{0:T(256)S(1)} %dynamic-update-slice), channel_id=1, replica_groups=mesh['dp'=16,'mp_0'=8,'mp_1'=2] {'dp','mp_0','mp_1'}, use_global_device_ids=true, to_apply=%add | all-reduce | flops 256 | bytes 2048
  440.2 0.7 broadcast_subtract_fusion
  (39 shorter events, 2.5 us)
Async XLA Ops:
  7.2 12.4 %copy-start = (bf16[512,2048]{1,0:T(8,128)(2,1)S(1)}, bf16[512,2048]{1,0:T(8,128)(2,1)}, u32[]{:S(2)}) copy-start(bf16[512,2048]{1,0:T(8,128)(2,1)} %param.4) | copy-start | bytes 6291460
  9.5 22.3 %all-to-all-start = ((bf16[16,1,1]{2,1,0:T(2,128)(2,1)}), bf16[16,1,1]{2,1,0:T(2,128)(2,1)S(1)}, u32[]{:S(2)}, u32[]{:S(2)}) async-start(bf16[16,1,1]{2,1,0:T(2,128)(2,1)} %copy.20), calls=%async_computation | async-start | bytes 16384 | tf_op jit(solution)/shard_map/all_to_all | solution.py:72
  31.8 190.5 %all-to-all-start.1 = ((bf16[16,1,128,2048]{3,2,1,0:T(8,128)(2,1)}), bf16[16,1,128,2048]{3,2,1,0:T(8,128)(2,1)}, u32[]{:S(2)}, u32[]{:S(2)}) async-start(bf16[16,1,128,2048]{3,2,1,0:T(8,128)(2,1)} %fusion.4), calls=%async_computation.1 | async-start | bytes 16777216 | tf_op jit(solution)/shard_map/all_to_all | solution.py:71
  38.9 319.9 %reduce-scatter.2.cloned.1.call-start = ((), (), s32[]{:S(2)}) async-start(), calls=%async_computation.3 | async-start | bytes 6684672 | tf_op jit(solution)/shard_map/reduce_scatter | solution.py:108
  232.8 30.5 %copy-start.1 = (f32[16,128,768]{2,1,0:T(8,128)}, f32[16,128,768]{2,1,0:T(8,128)S(1)}, u32[]{:S(2)}) copy-start(f32[16,128,768]{2,1,0:T(8,128)S(1)} %get-tuple-element.27) | copy-start | bytes 18874372
  275.2 0.7 copy-start.3
  275.2 165.1 %copy-start.2 = (f32[16,512]{1,0:T(8,128)S(1)}, f32[16,512]{1,0:T(8,128)}, u32[]{:S(2)}) copy-start(f32[16,512]{1,0:T(8,128)} %param.7) | copy-start | bytes 98308
Sparse Core Ops, SparseCore 0:
  275.3 83.5 reduce-scatter.1
where the time goes:
time: 448 us
  waiting for transfers between devices  223 us (50%)
  blocking collectives  139 us (31%)
  other arithmetic  23.1 us (5%)
  matrix products  22.3 us (5%)
  starting transfers between devices  17.1 us (4%)
  between operations  14.8 us (3%)
  local copies, waits for them, and re-layouts  7.87 us (2%)
    all_to_all x1, waiting for transfers between devices, on_device(): lax.all_to_all(outgoing, MP, split_axis=0, concat_axis=0, tiled=True)  180 us
    unnamed x2, blocking collectives  111 us
    reduce_scatter x1, waiting for transfers between devices, on_device(): lax.psum_scatter(weighted, 'dp', scatter_dimension=0, tiled=True)  43.5 us
    all_gather x2, blocking collectives, gathered_once(): both, at, found = (lax.all_gather(jnp.concatenate(lines), axis), 0, {})  28.3 us
    dot_general x1, matrix products, on_device(): jnp.einsum('sbik,sbif->kf', weight_half, got_rows, preferred_element_type...  11.8 us
    dot_general x1, matrix products, on_device(): jnp.einsum('sbif,kf->sbik', piece_rows, centroids, preferred_element_type...  10.5 us
    all_to_all x1, starting transfers between devices, on_device(): lax.all_to_all(slot_codes.astype(jnp.bfloat16), MP, split_axis=0, concat_...  9.97 us
  transfers between devices with their start and end apart: 3, of which 2 were waited for; matrix products, arithmetic and copies ran while one was open for 5% of the time, Pallas kernels for 0%

commit v1 on v0

v1 whole, which is shorter than its diff:
```python
import functools
import math

import jax
import jax.numpy as jnp
from jax import lax
from jax.experimental import pallas as pl
from jax.experimental.pallas import tpu as pltpu
from jax.sharding import PartitionSpec as P

BLOCK = 128
MESH = pl.DeviceIdType.MESH
NEG = -1e30
F32 = jnp.float32
BF16 = jnp.bfloat16


def rcopy(src, dst, ssem, rsem, dev):
    return pltpu.make_async_remote_copy(
        src_ref=src,
        dst_ref=dst,
        send_sem=ssem,
        recv_sem=rsem,
        device_id=dev,
        device_id_type=MESH,
    )


def kernel(
    data,
    cent,
    codes,
    lower,
    newc,
    shift,
    lognorm,
    newlow,
    full,
    got,
    part,
    selb,
    sel4,
    sc,
    wt,
    sums,
    r1,
    r2,
    r3,
    r4,
    tot,
    cv,
    ct,
    st,
    nrm,
    cnorm,
    cacc,
    cbuf,
    ccol,
    pa,
    pb,
    code_s,
    code_r,
    full_s,
    full_r,
    part_s,
    part_r,
    sel_s,
    sel_r,
    sel4_s,
    sel4_r,
    stat_s,
    stat_r,
    cnt_s,
    cnt_r,
    r1_s,
    r1_r,
    r2_s,
    r2_r,
    r3_s,
    r3_r,
    r4_s,
    r4_r,
    pa_s,
    pa_r,
    pb_s,
    pb_r,
):
    feat = data.shape[1]
    half = feat // 2
    width = cent.shape[0]
    own = width // 16
    sharp = 4.0 / math.sqrt(feat)
    p = lax.axis_index("dp")
    m = lax.axis_index("mp")
    z, c = m // 2, lax.rem(m, 2)
    y, x = p // 4, lax.rem(p, 4)

    def mp_of(dz, j):
        lane = c if j == 0 else 1 - c
        return lax.rem(z + dz + 8, 8) * 2 + lane

    def mp_dev(dz, j):
        return {"mp": mp_of(dz, j)}

    def rows(k, j):
        return pl.ds((k * 2 + j) * BLOCK, BLOCK)

    def slot(h, k, j):
        return got.at[h, rows(k, j), :]

    def mp_at(d):
        return lax.rem(m + d, 16)

    def dp_at(d):
        return lax.rem(p + d, 16)

    barrier = pltpu.get_barrier_semaphore()

    def greet(d, _):
        pl.semaphore_signal(barrier, inc=1, device_id={"mp": mp_at(d)}, device_id_type=MESH)
        pl.semaphore_signal(barrier, inc=1, device_id={"dp": dp_at(d)}, device_id_type=MESH)
        return _

    lax.fori_loop(1, 16, greet, 0)
    cv[m] = codes[...]
    pl.semaphore_wait(barrier, 30)

    order = ((0, 1), (1, 0))
    step = (1, -1)

    def full_copy(way, dist, h):
        src = data.at[:, h * half : (h + 1) * half] if dist == 0 else full.at[way, 0, h]
        return rcopy(
            src,
            full.at[way, dist, h],
            full_s.at[way, dist, h],
            full_r.at[way, dist, h],
            mp_dev(step[way], 0),
        )

    def code_copy(d):
        return rcopy(codes, cv.at[m], code_s.at[d], code_r.at[d], {"mp": mp_at(d)})

    def code_wait(d):
        src = lax.rem(m + 16 - d, 16)
        return rcopy(codes, cv.at[src], code_s.at[d], code_r.at[d], {"mp": src})

    lax.fori_loop(1, 16, lambda d, _: (code_copy(d).start(), _)[1], 0)
    for turn in range(2):
        for way in range(2):
            full_copy(way, 0, order[way][turn]).start()

    def block_of(g, s):
        return jnp.broadcast_to(cv[g, pl.ds(s, 1), :], (BLOCK, BLOCK)).astype(BF16)

    def choose(dst, src, code, first=0):
        for at in range(0, half, BLOCK):
            cols = slice(first + at, first + at + BLOCK)
            out = src[0:BLOCK, cols]
            for b in range(1, src.shape[0] // BLOCK):
                here = code == jnp.asarray(b + 1, BF16)
                out = jnp.where(here, src[b * BLOCK : (b + 1) * BLOCK, cols], out)
            dst[:, at : at + BLOCK] = out

    def part_copy(i, k, h):
        return rcopy(
            part.at[i, h], slot(h, k, 1), part_s.at[i, h], part_r.at[i, h], mp_dev(0, 1)
        )

    at_me, at_partner = block_of(m, m), block_of(m, mp_of(0, 1))
    for h in range(2):
        choose(part.at[0, h], data, at_partner, h * half)
        choose(slot(h, 0, 0), data, at_me, h * half)
    for h in range(2):
        part_copy(0, 0, h).start()

    square = jnp.square(cent[...].astype(F32))
    cnorm[...] = jnp.broadcast_to(jnp.sum(square, axis=1, keepdims=True), cnorm.shape)

    def wait_code(d, _):
        code_wait(d).wait_recv()
        return _

    lax.fori_loop(1, 16, wait_code, 0)

    def turn_codes(g, _):
        for s in range(16):
            ct[s, pl.ds(g, 1), :] = cv[g, s : s + 1, :]
        return _

    lax.fori_loop(0, 16, turn_codes, 0)

    def scores(k):
        where = pl.ds(pl.multiple_of(k * 256, 256), 256)
        nt = (((1,), (1,)), ((), ()))
        prod = lax.dot_general(
            cent[:, :half], got[0, where, :], nt, preferred_element_type=F32
        ) + lax.dot_general(cent[:, half:], got[1, where, :], nt, preferred_element_type=F32)
        score = sharp * (2.0 * prod - cnorm[:, 0:1])
        sc[k] = score
        best = jnp.max(score, axis=0, keepdims=True)
        mass = jnp.sum(jnp.exp(score - best), axis=0, keepdims=True)
        for j in range(2):
            g = mp_of(k, j)
            valid = ct[m, pl.ds(g, 1), :] > 0.0
            lanes = slice(j * BLOCK, (j + 1) * BLOCK)
            st[m, pl.ds(g, 1), :] = jnp.where(valid, best[:, lanes], NEG)
            st[m, pl.ds(16 + g, 1), :] = jnp.where(valid, mass[:, lanes], 0.0)

    def scores_at(ks):
        for k in ks:
            scores(k)

    def keep(way, dist, i, k, h):
        g = mp_of(-step[way] * (dist + 1), 0)
        for j, dst in enumerate((slot(h, k, 0), part.at[i, h])):
            choose(dst, full.at[way, dist, h], block_of(g, mp_of(0, j)))

    def onward(way, dz, j):
        return block_of(mp_of(-step[way] * 2, 0), mp_of(step[way] * dz, j))

    near = {0: 7, 1: 1}
    far = {0: 6, 1: 2}
    third = {0: 5, 1: 3}

    def sel_copy(way, j, h):
        return rcopy(
            selb.at[way, j, h],
            slot(h, third[way], j),
            sel_s.at[way, j, h],
            sel_r.at[way, j, h],
            mp_dev(step[way], j),
        )

    def sel4_copy(way, j):
        return rcopy(
            sel4.at[way, j],
            slot(order[way][0], 4, j),
            sel4_s.at[way, j],
            sel4_r.at[way, j],
            mp_dev(2 * step[way], j),
        )

    for turn in range(2):
        for way in range(2):
            h = order[way][turn]
            full_copy(way, 0, h).wait_recv()
            full_copy(way, 1, h).start()
    for way in range(2):
        for h in range(2):
            keep(way, 0, 1 + way, near[way], h)
        for h in range(2):
            part_copy(1 + way, near[way], h).start()
    for h in range(2):
        part_copy(0, 0, h).wait_recv()
    scores(0)
    for way in range(2):
        for h in range(2):
            part_copy(1 + way, near[way], h).wait_recv()
        scores(near[way])

    for turn in range(2):
        for way in range(2):
            h = order[way][turn]
            full_copy(way, 1, h).wait_recv()
            if turn == 0:
                for j in range(2):
                    choose(sel4.at[way, j], full.at[way, 1, h], onward(way, 2, j))
            for j in range(2):
                choose(selb.at[way, j, h], full.at[way, 1, h], onward(way, 1, j))
            keep(way, 1, 3 + way, far[way], h)
            if turn == 0:
                for j in range(2):
                    sel4_copy(way, j).start()
            for j in range(2):
                sel_copy(way, j, h).start()
            part_copy(3 + way, far[way], h).start()
    for way in range(2):
        for h in range(2):
            part_copy(3 + way, far[way], h).wait_recv()
        scores(far[way])
    for way in range(2):
        for j in range(2):
            sel4_copy(way, j).wait_recv()
    scores(4)
    for way in range(2):
        for j in range(2):
            for h in range(2):
                sel_copy(way, j, h).wait_recv()
        scores(third[way])

    def stat_copy(d):
        return rcopy(st.at[m], st.at[m], stat_s.at[d], stat_r.at[d], {"mp": mp_at(d)})

    def stat_wait(d, _):
        src = lax.rem(m + 16 - d, 16)
        rcopy(st.at[src], st.at[src], stat_s.at[d], stat_r.at[d], {"mp": src}).wait_recv()
        return _

    lax.fori_loop(1, 16, lambda d, _: (stat_copy(d).start(), _)[1], 0)
    lax.fori_loop(1, 16, stat_wait, 0)

    mine = ct[m]
    top = jnp.full(mine.shape, NEG, F32)
    for s in range(16):
        top = jnp.maximum(top, jnp.where(ct[s] == mine, st[s, 0:16, :], NEG))
    ceiling = jnp.maximum(top, 0.0)
    total = jnp.zeros(mine.shape, F32)
    for s in range(16):
        spread = st[s, 16:32, :] * jnp.exp(st[s, 0:16, :] - ceiling)
        total = total + jnp.where(ct[s] == mine, spread, 0.0)
    nrm[...] = ceiling + jnp.log(jnp.exp(-ceiling) + total)

    cacc[...] = jnp.zeros(cacc.shape, F32)

    def weigh(k, _):
        for j in range(2):
            g = mp_of(k, j)
            valid = ct[m, pl.ds(g, 1), :] > 0.0
            norm = nrm[pl.ds(g, 1), :]
            score = sc[k, :, j * BLOCK : (j + 1) * BLOCK]
            weight = jnp.where(valid, jnp.exp(score - norm), 0.0)
            cacc[...] += weight
            at = pl.multiple_of(k * 256 + j * BLOCK, BLOCK)
            wt[:, pl.ds(at, BLOCK)] = weight.astype(BF16)
        return _

    lax.fori_loop(0, 8, weigh, 0)

    quarters = half // 256

    def dp_dev(a, b):
        return {"dp": lax.rem(y + a + 4, 4) * 4 + lax.rem(x + b + 4, 4)}

    first = (x, y)
    second = (y, x)

    def first_dev(h, d):
        return dp_dev(0, d) if h == 0 else dp_dev(d, 0)

    def second_dev(h, d):
        return dp_dev(d, 0) if h == 0 else dp_dev(0, d)

    def plus(v, d):
        return lax.rem(v + d + 4, 4)

    def copy1(h, q, way):
        i = h * quarters + q
        src = sums.at[i, plus(first[h], 2), 2 * way : 2 * way + 2]
        return rcopy(src, r1.at[i, way], r1_s.at[i, way], r1_r.at[i, way], first_dev(h, step[way]))

    def copy2(h, q, way):
        i = h * quarters + q
        src = sums.at[i, plus(first[h], step[way])]
        return rcopy(src, r2.at[i, way], r2_s.at[i, way], r2_r.at[i, way], first_dev(h, step[way]))

    def copy3(h, q, way):
        i = h * quarters + q
        piece = pl.ds(way * (own // 2), own // 2)
        src = sums.at[i, first[h], plus(second[h], 2), piece]
        return rcopy(src, r3.at[i, way], r3_s.at[i, way], r3_r.at[i, way], second_dev(h, step[way]))

    def copy4(h, q, way):
        i = h * quarters + q
        src = sums.at[i, first[h], plus(second[h], step[way])]
        return rcopy(src, r4.at[i, way], r4_s.at[i, way], r4_r.at[i, way], second_dev(h, step[way]))

    def stage1(q):
        for h in range(2):
            i = h * quarters + q
            out = jnp.dot(
                wt[...], got[h, :, q * 256 : (q + 1) * 256], preferred_element_type=F32
            )
            for owner in range(16):
                yy, xx = owner // 4, owner % 4
                a, b = (xx, yy) if h == 0 else (yy, xx)
                sums[i, a, b] = out[owner * own : (owner + 1) * own]
            for way in range(2):
                copy1(h, q, way).start()

    def stage2(q):
        for h in range(2):
            i = h * quarters + q
            for way in range(2):
                copy1(h, q, way).wait_recv()
                a = plus(first[h], step[way])
                sums[i, a, 2 * way : 2 * way + 2] += r1[i, way]
                copy2(h, q, way).start()

    def stage3(q):
        for h in range(2):
            i = h * quarters + q
            for way in range(2):
                copy2(h, q, way).wait_recv()
            sums[i, first[h]] += r2[i, 0] + r2[i, 1]
            for way in range(2):
                copy3(h, q, way).start()

    def stage4(q):
        for h in range(2):
            i = h * quarters + q
            for way in range(2):
                copy3(h, q, way).wait_recv()
                b = plus(second[h], step[way])
                piece = pl.ds(way * (own // 2), own // 2)
                sums[i, first[h], b, piece] += r3[i, way]
                copy4(h, q, way).start()

    def finish(q):
        for h in range(2):
            i = h * quarters + q
            for way in range(2):
                copy4(h, q, way).wait_recv()
            cols = slice(h * half + q * 256, h * half + (q + 1) * 256)
            tot[:, cols] = sums[i, first[h], second[h]] + r4[i, 0] + r4[i, 1]

    def cnt_copy(d):
        return rcopy(cbuf.at[p], cbuf.at[p], cnt_s.at[d], cnt_r.at[d], {"dp": dp_at(d)})

    def cnt_wait(d, _):
        src = lax.rem(p + 16 - d, 16)
        rcopy(cbuf.at[src], cbuf.at[src], cnt_s.at[d], cnt_r.at[d], {"dp": src}).wait_recv()
        return _

    stages = (stage1, stage2, stage3, stage4, finish)
    for t in range(quarters + 4):
        for n, stage in enumerate(stages):
            if 0 <= t - n < quarters:
                stage(t - n)
        if t == 0:
            cbuf[p] = jnp.sum(cacc[...].T, axis=0, keepdims=True)
            lax.fori_loop(1, 16, lambda d, _: (cnt_copy(d).start(), _)[1], 0)
        if t == quarters:
            lax.fori_loop(1, 16, cnt_wait, 0)
            count = jnp.sum(cbuf[...], axis=0)
            ccol[...] = jnp.broadcast_to(count, (BLOCK, width)).T
            number = (lax.broadcasted_iota(jnp.int32, (4, BLOCK), 0) + 1).astype(F32)

            def own_top(s, v):
                here = ct[s, pl.ds(m, 1), :] == number
                return jnp.maximum(v, jnp.where(here, st[s, pl.ds(m, 1), :], NEG))

            best = lax.fori_loop(0, 16, own_top, jnp.full((4, BLOCK), NEG, F32))
            roof = jnp.maximum(best, 0.0)

            def own_mass(s, v):
                here = ct[s, pl.ds(m, 1), :] == number
                spread = st[s, pl.ds(16 + m, 1), :] * jnp.exp(st[s, pl.ds(m, 1), :] - roof)
                return v + jnp.where(here, spread, 0.0)

            mass = lax.fori_loop(0, 16, own_mass, jnp.zeros((4, BLOCK), F32))
            lognorm[...] = roof + jnp.log(jnp.exp(-roof) + mass)

    mine_rows = pl.ds(pl.multiple_of(p * own, own), own)
    old = cent[mine_rows, :].astype(F32)
    denom = ccol[mine_rows, 0:1] + 1.0
    updated = (tot[...] + old) / denom
    newc[...] = updated
    move = jnp.sqrt(jnp.sum(jnp.square(updated - old), axis=1, keepdims=True) + 1.0)
    wide = jnp.broadcast_to(move, (own, BLOCK))
    pa[p] = jnp.max(wide, axis=0, keepdims=True)

    def pa_copy(d):
        return rcopy(pa.at[p], pa.at[p], pa_s.at[d], pa_r.at[d], {"dp": dp_at(d)})

    def pa_wait(d, _):
        src = lax.rem(p + 16 - d, 16)
        rcopy(pa.at[src], pa.at[src], pa_s.at[d], pa_r.at[d], {"dp": src}).wait_recv()
        return _

    lax.fori_loop(1, 16, lambda d, _: (pa_copy(d).start(), _)[1], 0)
    tall = jnp.concatenate([wide, jnp.zeros((BLOCK - own, BLOCK), F32)], axis=0)
    shift[...] = tall.T[0:1, :]
    lax.fori_loop(1, 16, pa_wait, 0)
    pb[m] = jnp.max(pa[...], axis=0)

    def pb_copy(d):
        return rcopy(pb.at[m], pb.at[m], pb_s.at[d], pb_r.at[d], {"mp": mp_at(d)})

    def pb_wait(d, _):
        src = lax.rem(m + 16 - d, 16)
        rcopy(pb.at[src], pb.at[src], pb_s.at[d], pb_r.at[d], {"mp": src}).wait_recv()
        return _

    lax.fori_loop(1, 16, lambda d, _: (pb_copy(d).start(), _)[1], 0)

    for way in range(2):
        for dist in range(2):
            for h in range(2):
                full_copy(way, dist, h).wait_send()
        for j in range(2):
            sel4_copy(way, j).wait_send()
            for h in range(2):
                sel_copy(way, j, h).wait_send()
    for i in range(5):
        for h in range(2):
            part_copy(i, 0, h).wait_send()
    for q in range(quarters):
        for h in range(2):
            for way in range(2):
                for copy in (copy1, copy2, copy3, copy4):
                    copy(h, q, way).wait_send()

    def sent(d, _):
        for copy in (code_copy, stat_copy, cnt_copy, pa_copy):
            copy(d).wait_send()
        return _

    lax.fori_loop(1, 16, sent, 0)
    lax.fori_loop(1, 16, pb_wait, 0)
    for s in range(16):
        peak = pb[s]
        newlow[s : s + 1, :] = lower[s : s + 1, :] - jnp.concatenate([peak] * 4, axis=1)
    lax.fori_loop(1, 16, lambda d, _: (pb_copy(d).wait_send(), _)[1], 0)


def on_device(data_rows, centroids, block_mask, lower_bound):
    rows, feat = data_rows.shape
    blocks = rows // BLOCK
    width = centroids.shape[0]
    half = feat // 2
    own = width // 16
    labels = jnp.arange(1, blocks + 1, dtype=jnp.int32)
    codes = jnp.sum(block_mask * labels[None, :], axis=1, dtype=jnp.int32)
    codes = jnp.broadcast_to(codes[:, None], (16, BLOCK)).astype(F32)
    items = feat // 256
    dma = pltpu.SemaphoreType.DMA
    vmem = pltpu.VMEM
    updated, movement, log_norm, new_lower = pl.pallas_call(
        kernel,
        name="kmeans_step",
        out_shape=(
            jax.ShapeDtypeStruct((own, feat), F32),
            jax.ShapeDtypeStruct((1, BLOCK), F32),
            jax.ShapeDtypeStruct((blocks, BLOCK), F32),
            jax.ShapeDtypeStruct(lower_bound.shape, F32),
        ),
        in_specs=[pl.BlockSpec(memory_space=vmem)] * 4,
        out_specs=[pl.BlockSpec(memory_space=vmem)] * 4,
        scratch_shapes=[
            vmem((2, 2, 2, rows, half), BF16),
            vmem((2, 16 * BLOCK, half), BF16),
            vmem((5, 2, BLOCK, half), BF16),
            vmem((2, 2, 2, BLOCK, half), BF16),
            vmem((2, 2, BLOCK, half), BF16),
            vmem((8, width, 2 * BLOCK), F32),
            vmem((width, 16 * BLOCK), BF16),
            vmem((items, 4, 4, own, 256), F32),
            vmem((items, 2, 2, own, 256), F32),
            vmem((items, 2, 4, own, 256), F32),
            vmem((items, 2, own // 2, 256), F32),
            vmem((items, 2, own, 256), F32),
            vmem((own, feat), F32),
            vmem((16, 16, BLOCK), F32),
            vmem((16, 16, BLOCK), F32),
            vmem((16, 32, BLOCK), F32),
            vmem((16, BLOCK), F32),
            vmem((width, BLOCK), F32),
            vmem((width, BLOCK), F32),
            vmem((16, 1, width), F32),
            vmem((width, BLOCK), F32),
            vmem((16, 1, BLOCK), F32),
            vmem((16, 1, BLOCK), F32),
            dma((16,)),
            dma((16,)),
            dma((2, 2, 2)),
            dma((2, 2, 2)),
            dma((5, 2)),
            dma((5, 2)),
            dma((2, 2, 2)),
            dma((2, 2, 2)),
            dma((2, 2)),
            dma((2, 2)),
            dma((16,)),
            dma((16,)),
            dma((16,)),
            dma((16,)),
            *[dma((items, 2)) for _ in range(8)],
            *[dma((16,)) for _ in range(4)],
        ],
        compiler_params=pltpu.CompilerParams(
            collective_id=0, has_side_effects=True, vmem_limit_bytes=66_000_000
        ),
    )(data_rows, centroids, codes, lower_bound)
    return updated, movement[0, :own], log_norm.reshape(-1), new_lower


def solution(mesh):
    in_specs = (
        P(("dp", "mp"), None),
        P("mp", None),
        P(None, ("dp", "mp")),
        P(None, ("dp", "mp")),
    )
    out_specs = (
        P(("mp", "dp"), None),
        P(("mp", "dp")),
        P(("dp", "mp")),
        P(None, ("dp", "mp")),
    )
    return jax.shard_map(
        on_device, mesh=mesh, in_specs=in_specs, out_specs=out_specs, check_vma=False
    )
```

time: 448 us -> 232 us (0.52)
  Pallas kernels: 0 us -> 224 us
  waiting for transfers between devices: 223 us -> 0 us
  blocking collectives: 139 us -> 0 us
  other arithmetic: 23.1 us -> 0.78 us
  matrix products: 22.3 us -> 0 us
  starting transfers between devices: 17.1 us -> 0 us
  between operations: 14.8 us -> 0.65 us
    pallas_call x0 -> x1, Pallas kernels: none -> 224 us  [on_device(): pl.pallas_call(kernel, name='kmeans_step', out_shape=(jax.ShapeDtypeStruc...]
    all_to_all x2 -> x0, waiting for transfers between devices: 180 us -> none  [the longest x1 180 us: on_device(): lax.all_to_all(outgoing, MP, split_axis=0, concat_axis=0, tiled=True)]
    unnamed x2 -> x0, blocking collectives: 111 us -> none
    reduce_scatter x1 -> x0, waiting for transfers between devices: 43.5 us -> none  [on_device(): lax.psum_scatter(weighted, 'dp', scatter_dimension=0, tiled=True)]
    all_gather x2 -> x0, blocking collectives: 28.3 us -> none  [gathered_once(): both, at, found = (lax.all_gather(jnp.concatenate(lines), axis), 0, {})]
    dot_general x2 -> x0, matrix products: 22.3 us -> none  [the longest x1 11.8 us: on_device(): jnp.einsum('sbik,sbif->kf', weight_half, got_rows, preferred_element_type...]
    all_to_all x2 -> x0, starting transfers between devices: 17.1 us -> none  [the longest x1 9.97 us: on_device(): lax.all_to_all(slot_codes.astype(jnp.bfloat16), MP, split_axis=0, concat_...]
    reduce_sum x6 -> x1, other arithmetic: 11 us -> 0.77 us  [on_device(): codes = jnp.sum(block_mask * labels[None, :], axis=1, dtype=jnp.int32)]
  transfers between devices with their start and end apart: 3 -> 0, of which waited for: 2 -> 0; matrix products, arithmetic and copies ran while one was open for 5% -> 0% of each run, Pallas kernels for 0% -> 0%
where the time goes in v1:
time: 232 us; the launch traced here: 231 us
  Pallas kernels  224 us (97%)
  local copies, waits for them, and re-layouts  6.19 us (3%)
    pallas_call x1, Pallas kernels, on_device(): pl.pallas_call(kernel, name='kmeans_step', out_shape=(jax.ShapeDtypeStruc...  224 us

profile of v1, /device:TPU:1, one launch (start us, length us, event | category | flops | bytes accessed | tf_op | source)
XLA Modules:
  0.0 231.3 jit_solution(13430265010363700843)
XLA Ops:
  0.6 0.8 multiply_reduce_fusion
  1.4 0.7 broadcast_in_dim.2.codes
  2.1 223.7 %kmeans_step.1 = (f32[48,2048]{1,0:T(8,128)}, f32[1,128]{1,0:T(1,128)}, f32[4,128]{1,0:T(4,128)}, f32[16,512]{1,0:T(8,128)}) custom-call(bf16[512,2048]{1,0:T(8,128)(2,1)} %data.1, bf16[768,2048]{1,0:T(8,128)(2,1)} %cent.1, f32[16,128]{1,0:T(8,128)} %broadcast_in_dim.2.codes, f32[16,512]{1,0:T(8,128)} %lower.1), custom_call_target="tpu_custom_call" | custom-call | tf_op jit(solution)/shard_map/kmeans_step/pallas_call | solution.py:529
  225.8 1.1 slice_bitcast_fusion
  226.9 1.8 copy.11
  228.7 1.3 copy.12
  229.9 1.4 copy.13
  (2 shorter events, 0.0 us)

commit v2 on v1

v2 whole, which is shorter than its diff:
```python
import functools
import math

import jax
import jax.numpy as jnp
from jax import lax
from jax.experimental import pallas as pl
from jax.experimental.pallas import tpu as pltpu
from jax.sharding import PartitionSpec as P

BLOCK = 128
MESH = pl.DeviceIdType.MESH
NEG = -1e30
F32 = jnp.float32
BF16 = jnp.bfloat16


def rcopy(src, dst, ssem, rsem, dev):
    return pltpu.make_async_remote_copy(
        src_ref=src,
        dst_ref=dst,
        send_sem=ssem,
        recv_sem=rsem,
        device_id=dev,
        device_id_type=MESH,
    )


def kernel(
    data_in,
    cent_in,
    mask_in,
    newc,
    shift,
    lognorm,
    peaks,
    data,
    cent,
    mask,
    full,
    got,
    part,
    selb,
    sel4,
    sc,
    wt,
    sums,
    r1,
    r2,
    r3,
    r4,
    tot,
    cm,
    cv,
    ct,
    st,
    tops,
    nrm,
    cnorm,
    cacc,
    cbuf,
    ccol,
    pa,
    load_s,
    code_s,
    code_r,
    full_s,
    full_r,
    part_s,
    part_r,
    sel_s,
    sel_r,
    sel4_s,
    sel4_r,
    stat_s,
    stat_r,
    cnt_s,
    cnt_r,
    r1_s,
    r1_r,
    r2_s,
    r2_r,
    r3_s,
    r3_r,
    r4_s,
    r4_r,
    pa_s,
    pa_r,
    pb_s,
    pb_r,
):
    half = data.shape[2]
    feat = 2 * half
    width = cent.shape[0]
    own = width // 16
    sharp = 4.0 / math.sqrt(feat)
    p = lax.axis_index("dp")
    m = lax.axis_index("mp")
    z, c = m // 2, lax.rem(m, 2)
    y, x = p // 4, lax.rem(p, 4)

    def mp_of(dz, j):
        lane = c if j == 0 else 1 - c
        return lax.rem(z + dz + 8, 8) * 2 + lane

    def mp_dev(dz, j):
        return {"mp": mp_of(dz, j)}

    def rows(k, j):
        return pl.ds((k * 2 + j) * BLOCK, BLOCK)

    def slot(h, k, j):
        return got.at[h, rows(k, j), :]

    def mp_at(d):
        return lax.rem(m + d, 16)

    def dp_at(d):
        return lax.rem(p + d, 16)

    barrier = pltpu.get_barrier_semaphore()

    def greet(d, _):
        pl.semaphore_signal(barrier, inc=1, device_id={"mp": mp_at(d)}, device_id_type=MESH)
        pl.semaphore_signal(barrier, inc=1, device_id={"dp": dp_at(d)}, device_id_type=MESH)
        return _

    loads = [pltpu.make_async_copy(mask_in, mask, load_s.at[0])]
    for h in range(2):
        src = data_in.at[:, h * half : (h + 1) * half]
        loads.append(pltpu.make_async_copy(src, data.at[h], load_s.at[1 + h]))
    loads.append(pltpu.make_async_copy(cent_in, cent, load_s.at[3]))
    for load in loads:
        load.start()
    lax.fori_loop(1, 16, greet, 0)

    loads[0].wait()
    label = (lax.broadcasted_iota(jnp.int32, mask.shape, 0) + 1).astype(F32)
    code = jnp.sum(mask[...].astype(F32) * label, axis=0, keepdims=True)
    cv[m] = code
    shards = lax.broadcasted_iota(jnp.int32, code.shape, 1)
    for j in range(2):
        here = jnp.sum(jnp.where(shards == mp_of(0, j), code, 0.0), axis=1, keepdims=True)
        cm[j : j + 1, :] = jnp.broadcast_to(here, (1, BLOCK))
    for load in loads[1:3]:
        load.wait()
    pl.semaphore_wait(barrier, 30)

    order = ((0, 1), (1, 0))
    step = (1, -1)

    def full_copy(way, dist, h):
        src = data.at[h] if dist == 0 else full.at[way, 0, h]
        return rcopy(
            src,
            full.at[way, dist, h],
            full_s.at[way, dist, h],
            full_r.at[way, dist, h],
            mp_dev(step[way], 0),
        )

    def code_copy(d):
        return rcopy(cv.at[m], cv.at[m], code_s.at[d], code_r.at[d], {"mp": mp_at(d)})

    def code_wait(d):
        src = lax.rem(m + 16 - d, 16)
        return rcopy(cv.at[src], cv.at[src], code_s.at[d], code_r.at[d], {"mp": src})

    lax.fori_loop(1, 16, lambda d, _: (code_copy(d).start(), _)[1], 0)
    for turn in range(2):
        for way in range(2):
            full_copy(way, 0, order[way][turn]).start()

    def choose(dst, src, code):
        code = jnp.broadcast_to(code, (BLOCK, BLOCK)).astype(BF16)
        for at in range(0, half, BLOCK):
            cols = slice(at, at + BLOCK)
            out = src[0:BLOCK, cols]
            for b in range(1, src.shape[0] // BLOCK):
                here = code == jnp.asarray(b + 1, BF16)
                out = jnp.where(here, src[b * BLOCK : (b + 1) * BLOCK, cols], out)
            dst[:, at : at + BLOCK] = out

    def part_copy(i, k, h):
        return rcopy(
            part.at[i, h], slot(h, k, 1), part_s.at[i, h], part_r.at[i, h], mp_dev(0, 1)
        )

    for h in range(2):
        choose(part.at[0, h], data.at[h], cm[1:2, :])
        choose(slot(h, 0, 0), data.at[h], cm[0:1, :])
    for h in range(2):
        part_copy(0, 0, h).start()

    loads[3].wait()
    square = jnp.square(cent[...].astype(F32))
    cnorm[...] = jnp.broadcast_to(jnp.sum(square, axis=1, keepdims=True), cnorm.shape)

    def wait_code(d, _):
        code_wait(d).wait_recv()
        return _

    lax.fori_loop(1, 16, wait_code, 0)

    codes = cv[:, 0, :]
    for s in range(16):
        column = jnp.broadcast_to(codes[:, s : s + 1], (16, BLOCK))
        for zg in range(8):
            ct[s, zg] = column[2 * zg : 2 * zg + 2]

    def lane_of(j):
        return pl.ds(c if j == 0 else 1 - c, 1)

    def code_of(dz, j, shard):
        return ct[shard, lax.rem(z + dz + 8, 8), lane_of(j), :]

    place = (2, 3, 4, 6, 5, 7, 0, 1)

    def place_of(k):
        at = lax.rem(k + 10, 8)
        return at + jnp.where(at == 5, 1, 0) - jnp.where(at == 6, 1, 0)

    def product(k, h):
        return lax.dot_general(
            cent[:, h * half : (h + 1) * half],
            got[h, k * 256 : (k + 1) * 256, :],
            (((1,), (1,)), ((), ())),
            preferred_element_type=F32,
        )

    def weigh_up(k, prod):
        score = sharp * (2.0 * prod - cnorm[:, 0:1])
        best = jnp.max(score, axis=0, keepdims=True)
        power = jnp.exp(score - best)
        sc[k] = power
        mass = jnp.sum(power, axis=0, keepdims=True)
        whole = best + jnp.log(mass)
        for j in range(2):
            valid = code_of(k, j, m) > 0.0
            lanes = slice(j * BLOCK, (j + 1) * BLOCK)
            tops[k, lane_of(j), :] = best[:, lanes]
            st[m, place[k], lane_of(j), :] = jnp.where(valid, whole[:, lanes], NEG)

    def scores(k):
        weigh_up(k, product(k, 0) + product(k, 1))

    def keep(way, dist, i, k, h):
        for j, dst in enumerate((slot(h, k, 0), part.at[i, h])):
            choose(dst, full.at[way, dist, h], code_of(-step[way] * (dist + 1), 0, mp_of(0, j)))

    def onward(way, dz, j):
        return code_of(-step[way] * 2, 0, mp_of(step[way] * dz, j))

    near = {0: 7, 1: 1}
    far = {0: 6, 1: 2}
    third = {0: 5, 1: 3}

    def sel_copy(way, j, h):
        return rcopy(
            selb.at[way, j, h],
            slot(h, third[way], j),
            sel_s.at[way, j, h],
            sel_r.at[way, j, h],
            mp_dev(step[way], j),
        )

    def sel4_copy(way, j):
        return rcopy(
            sel4.at[way, j],
            slot(order[way][0], 4, j),
            sel4_s.at[way, j],
            sel4_r.at[way, j],
            mp_dev(2 * step[way], j),
        )

    for turn in range(2):
        for way in range(2):
            h = order[way][turn]
            full_copy(way, 0, h).wait_recv()
            full_copy(way, 1, h).start()
    for way in range(2):
        for h in range(2):
            keep(way, 0, 1 + way, near[way], h)
        for h in range(2):
            part_copy(1 + way, near[way], h).start()
    for h in range(2):
        part_copy(0, 0, h).wait_recv()
    scores(0)
    for way in range(2):
        for h in range(2):
            part_copy(1 + way, near[way], h).wait_recv()
        scores(near[way])

    for turn in range(2):
        for way in range(2):
            h = order[way][turn]
            full_copy(way, 1, h).wait_recv()
            if turn == 0:
                for j in range(2):
                    choose(sel4.at[way, j], full.at[way, 1, h], onward(way, 2, j))
            for j in range(2):
                choose(selb.at[way, j, h], full.at[way, 1, h], onward(way, 1, j))
            keep(way, 1, 3 + way, far[way], h)
            if turn == 0:
                for j in range(2):
                    sel4_copy(way, j).start()
            part_copy(3 + way, far[way], h).start()
            for j in range(2 - turn):
                sel_copy(way, j, h).start()
    for way in range(2):
        for h in range(2):
            part_copy(3 + way, far[way], h).wait_recv()
        scores(far[way])
    parts = (slice(0, 6), slice(6, 8))

    def stat_copy(n, d):
        ref = st.at[m, parts[n]]
        return rcopy(ref, ref, stat_s.at[n, d], stat_r.at[n, d], {"mp": mp_at(d)})

    def stat_wait(n, d):
        src = lax.rem(m + 16 - d, 16)
        ref = st.at[src, parts[n]]
        rcopy(ref, ref, stat_s.at[n, d], stat_r.at[n, d], {"mp": src}).wait_recv()

    for way in range(2):
        for j in range(2):
            sel4_copy(way, j).wait_recv()
    scores(4)
    lax.fori_loop(1, 16, lambda d, _: (stat_copy(0, d).start(), _)[1], 0)
    for way in range(2):
        sel_copy(way, 1, order[way][1]).start()
    for turn in range(2):
        for way in range(2):
            h = order[way][turn]
            for j in range(2):
                sel_copy(way, j, h).wait_recv()
            prod = product(third[way], h)
            if turn == 0:
                sc[third[way]] = prod
            else:
                weigh_up(third[way], sc[third[way]] + prod)
    lax.fori_loop(1, 16, lambda d, _: (stat_copy(1, d).start(), _)[1], 0)

    def stats_wait(d, _):
        stat_wait(0, d)
        stat_wait(1, d)
        return _

    lax.fori_loop(1, 16, stats_wait, 0)

    def log_sum(pieces):
        top = functools.reduce(jnp.maximum, pieces)
        ceiling = jnp.maximum(top, 0.0)
        total = functools.reduce(jnp.add, [jnp.exp(piece - ceiling) for piece in pieces])
        return ceiling + jnp.log(jnp.exp(-ceiling) + total)

    def combine(zg, _):
        mine = ct[m, zg]
        pieces = [
            jnp.where(ct[s, zg] == mine, st[s, place_of(zg - s // 2)], NEG) for s in range(16)
        ]
        k = lax.rem(zg - z + 8, 8)
        nrm[zg] = jnp.where(mine > 0.0, jnp.exp(tops[k] - log_sum(pieces)), 0.0)
        return _

    lax.fori_loop(0, 8, combine, 0)

    for k in range(8):
        for j in range(2):
            lanes = slice(j * BLOCK, (j + 1) * BLOCK)
            scale = nrm[lax.rem(z + k, 8), lane_of(j), :]
            weight = sc[k, :, lanes] * scale
            if k == 0 and j == 0:
                cacc[...] = weight
            else:
                cacc[...] += weight
            wt[:, k * 256 + j * BLOCK : k * 256 + (j + 1) * BLOCK] = weight.astype(BF16)

    quarters = half // 256
    items = 2 * quarters

    def dp_dev(a, b):
        return {"dp": lax.rem(y + a + 4, 4) * 4 + lax.rem(x + b + 4, 4)}

    first = (x, y)
    second = (y, x)

    def first_dev(h, d):
        return dp_dev(0, d) if h == 0 else dp_dev(d, 0)

    def second_dev(h, d):
        return dp_dev(d, 0) if h == 0 else dp_dev(0, d)

    def plus(v, d):
        return lax.rem(v + d + 4, 4)

    def copy1(i, way):
        h = i % 2
        src = sums.at[i, plus(first[h], 2), 2 * way : 2 * way + 2]
        return rcopy(src, r1.at[i, way], r1_s.at[i, way], r1_r.at[i, way], first_dev(h, step[way]))

    def copy2(i, way):
        h = i % 2
        src = sums.at[i, plus(first[h], step[way])]
        return rcopy(src, r2.at[i, way], r2_s.at[i, way], r2_r.at[i, way], first_dev(h, step[way]))

    def copy3(i, way):
        h = i % 2
        piece = pl.ds(way * (own // 2), own // 2)
        src = sums.at[i, first[h], plus(second[h], 2), piece]
        return rcopy(src, r3.at[i, way], r3_s.at[i, way], r3_r.at[i, way], second_dev(h, step[way]))

    def copy4(i, way):
        h = i % 2
        src = sums.at[i, first[h], plus(second[h], step[way])]
        return rcopy(src, r4.at[i, way], r4_s.at[i, way], r4_r.at[i, way], second_dev(h, step[way]))

    def stage1(i):
        h, q = i % 2, i // 2
        out = jnp.dot(wt[...], got[h, :, q * 256 : (q + 1) * 256], preferred_element_type=F32)
        for owner in range(16):
            yy, xx = owner // 4, owner % 4
            a, b = (xx, yy) if h == 0 else (yy, xx)
            sums[i, a, b] = out[owner * own : (owner + 1) * own]
        for way in range(2):
            copy1(i, way).start()

    def stage2(i):
        for way in range(2):
            copy1(i, way).wait_recv()
            a = plus(first[i % 2], step[way])
            sums[i, a, 2 * way : 2 * way + 2] += r1[i, way]
            copy2(i, way).start()

    def stage3(i):
        for way in range(2):
            copy2(i, way).wait_recv()
        sums[i, first[i % 2]] += r2[i, 0] + r2[i, 1]
        for way in range(2):
            copy3(i, way).start()

    def stage4(i):
        h = i % 2
        for way in range(2):
            copy3(i, way).wait_recv()
            b = plus(second[h], step[way])
            piece = pl.ds(way * (own // 2), own // 2)
            sums[i, first[h], b, piece] += r3[i, way]
            copy4(i, way).start()

    def finish(i):
        h, q = i % 2, i // 2
        for way in range(2):
            copy4(i, way).wait_recv()
        cols = slice(h * half + q * 256, h * half + (q + 1) * 256)
        tot[:, cols] = sums[i, first[h], second[h]] + r4[i, 0] + r4[i, 1]

    def cnt_copy(d):
        return rcopy(cbuf.at[p], cbuf.at[p], cnt_s.at[d], cnt_r.at[d], {"dp": dp_at(d)})

    def cnt_wait(d, _):
        src = lax.rem(p + 16 - d, 16)
        rcopy(cbuf.at[src], cbuf.at[src], cnt_s.at[d], cnt_r.at[d], {"dp": src}).wait_recv()
        return _

    stages = ((stage1, 0), (stage2, 2), (stage3, 6), (stage4, 8), (finish, 10))
    for t in range(items + 10):
        for stage, late in stages:
            if 0 <= t - late < items:
                stage(t - late)
        if t == 1:
            cbuf[p] = jnp.sum(cacc[...].T, axis=0, keepdims=True)
            lax.fori_loop(1, 16, lambda d, _: (cnt_copy(d).start(), _)[1], 0)
        if t == items - 1:
            lax.fori_loop(1, 16, cnt_wait, 0)
            count = jnp.sum(cbuf[...], axis=0)
            ccol[...] = jnp.broadcast_to(count, (BLOCK, width)).T
            number = (lax.broadcasted_iota(jnp.int32, (4, BLOCK), 0) + 1).astype(F32)
            pieces = []
            for s in range(16):
                here = ct[s, z, lane_of(0), :] == number
                piece = st[s, place_of(z - s // 2), lane_of(0), :]
                pieces.append(jnp.where(here, piece, NEG))
            lognorm[...] = log_sum(pieces)

    mine_rows = pl.ds(pl.multiple_of(p * own, own), own)
    old = cent[mine_rows, :].astype(F32)
    denom = ccol[mine_rows, 0:1] + 1.0
    updated = (tot[...] + old) / denom
    newc[...] = updated
    move = jnp.sqrt(jnp.sum(jnp.square(updated - old), axis=1, keepdims=True) + 1.0)
    wide = jnp.broadcast_to(move, (own, BLOCK))
    pa[p] = jnp.max(wide, axis=0, keepdims=True)

    def pa_copy(d):
        return rcopy(pa.at[p], pa.at[p], pa_s.at[d], pa_r.at[d], {"dp": dp_at(d)})

    def pa_wait(d, _):
        src = lax.rem(p + 16 - d, 16)
        rcopy(pa.at[src], pa.at[src], pa_s.at[d], pa_r.at[d], {"dp": src}).wait_recv()
        return _

    lax.fori_loop(1, 16, lambda d, _: (pa_copy(d).start(), _)[1], 0)
    tall = jnp.concatenate([wide, jnp.zeros((BLOCK - own, BLOCK), F32)], axis=0)
    shift[...] = tall.T[0:1, :]
    lax.fori_loop(1, 16, pa_wait, 0)
    peaks[m] = jnp.max(pa[...], axis=0)

    def pb_copy(d):
        return rcopy(peaks.at[m], peaks.at[m], pb_s.at[d], pb_r.at[d], {"mp": mp_at(d)})

    def pb_wait(d, _):
        src = lax.rem(m + 16 - d, 16)
        rcopy(peaks.at[src], peaks.at[src], pb_s.at[d], pb_r.at[d], {"mp": src}).wait_recv()
        return _

    lax.fori_loop(1, 16, lambda d, _: (pb_copy(d).start(), _)[1], 0)

    for way in range(2):
        for dist in range(2):
            for h in range(2):
                full_copy(way, dist, h).wait_send()
        for j in range(2):
            sel4_copy(way, j).wait_send()
            for h in range(2):
                sel_copy(way, j, h).wait_send()
    for i in range(5):
        for h in range(2):
            part_copy(i, 0, h).wait_send()
    for i in range(items):
        for way in range(2):
            for copy in (copy1, copy2, copy3, copy4):
                copy(i, way).wait_send()

    def sent(d, _):
        for copy in (code_copy, cnt_copy, pa_copy):
            copy(d).wait_send()
        for n in range(2):
            stat_copy(n, d).wait_send()
        return _

    lax.fori_loop(1, 16, sent, 0)
    lax.fori_loop(1, 16, pb_wait, 0)
    lax.fori_loop(1, 16, lambda d, _: (pb_copy(d).wait_send(), _)[1], 0)


def outputs(made, width, logs, peaks, lower, newc, shift, lognorm, newlow):
    newc[...] = made[...]
    shift[...] = width[:, : shift.shape[1]]
    lognorm[...] = logs[...]
    for s in range(16):
        newlow[s : s + 1, :] = lower[s : s + 1, :] - jnp.concatenate([peaks[s]] * 4, axis=1)


def on_device(data_rows, centroids, block_mask, lower_bound):
    rows, feat = data_rows.shape
    blocks = rows // BLOCK
    width = centroids.shape[0]
    half = feat // 2
    own = width // 16
    items = feat // 256
    dma = pltpu.SemaphoreType.DMA
    vmem = pltpu.VMEM
    made, movement, log_norm, peaks = pl.pallas_call(
        kernel,
        name="kmeans_step",
        out_shape=(
            jax.ShapeDtypeStruct((own, feat), F32),
            jax.ShapeDtypeStruct((1, BLOCK), F32),
            jax.ShapeDtypeStruct((blocks, BLOCK), F32),
            jax.ShapeDtypeStruct((16, 1, BLOCK), F32),
        ),
        in_specs=[pl.BlockSpec(memory_space=pl.ANY)] * 3,
        out_specs=[pl.BlockSpec(memory_space=vmem)] * 4,
        scratch_shapes=[
            vmem((2, rows, half), BF16),
            vmem((width, feat), BF16),
            vmem((blocks, 16), jnp.int32),
            vmem((2, 2, 2, rows, half), BF16),
            vmem((2, 16 * BLOCK, half), BF16),
            vmem((5, 2, BLOCK, half), BF16),
            vmem((2, 2, 2, BLOCK, half), BF16),
            vmem((2, 2, BLOCK, half), BF16),
            vmem((8, width, 2 * BLOCK), F32),
            vmem((width, 16 * BLOCK), BF16),
            vmem((items, 4, 4, own, 256), F32),
            vmem((items, 2, 2, own, 256), F32),
            vmem((items, 2, 4, own, 256), F32),
            vmem((items, 2, own // 2, 256), F32),
            vmem((items, 2, own, 256), F32),
            vmem((own, feat), F32),
            vmem((2, BLOCK), F32),
            vmem((16, 1, 16), F32),
            vmem((16, 8, 2, BLOCK), F32),
            vmem((16, 8, 2, BLOCK), F32),
            vmem((8, 2, BLOCK), F32),
            vmem((8, 2, BLOCK), F32),
            vmem((width, BLOCK), F32),
            vmem((width, BLOCK), F32),
            vmem((16, 1, width), F32),
            vmem((width, BLOCK), F32),
            vmem((16, 1, BLOCK), F32),
            dma((4,)),
            dma((16,)),
            dma((16,)),
            dma((2, 2, 2)),
            dma((2, 2, 2)),
            dma((5, 2)),
            dma((5, 2)),
            dma((2, 2, 2)),
            dma((2, 2, 2)),
            dma((2, 2)),
            dma((2, 2)),
            dma((2, 16)),
            dma((2, 16)),
            dma((16,)),
            dma((16,)),
            *[dma((items, 2)) for _ in range(8)],
            *[dma((16,)) for _ in range(4)],
        ],
        compiler_params=pltpu.CompilerParams(
            collective_id=0, has_side_effects=True, vmem_limit_bytes=66_000_000
        ),
    )(data_rows, centroids, block_mask.T)
    updated, movement, log_norm, new_lower = pl.pallas_call(
        outputs,
        name="outputs",
        out_shape=(
            jax.ShapeDtypeStruct(made.shape, F32),
            jax.ShapeDtypeStruct((1, own), F32),
            jax.ShapeDtypeStruct(log_norm.shape, F32),
            jax.ShapeDtypeStruct(lower_bound.shape, F32),
        ),
        in_specs=[pl.BlockSpec(memory_space=vmem)] * 5,
        out_specs=[pl.BlockSpec(memory_space=vmem)] * 4,
    )(made, movement, log_norm, peaks, lower_bound)
    return updated, movement.reshape(-1), log_norm.reshape(-1), new_lower


def solution(mesh):
    in_specs = (
        P(("dp", "mp"), None),
        P("mp", None),
        P(None, ("dp", "mp")),
        P(None, ("dp", "mp")),
    )
    out_specs = (
        P(("mp", "dp"), None),
        P(("mp", "dp")),
        P(("dp", "mp")),
        P(None, ("dp", "mp")),
    )
    return jax.shard_map(
        on_device, mesh=mesh, in_specs=in_specs, out_specs=out_specs, check_vma=False
    )
```

time: 232 us -> 218 us (0.940)
  Pallas kernels: 224 us -> 217 us
  local copies, waits for them, and re-layouts: 6.19 us -> 0 us
    pallas_call x1, Pallas kernels: 224 us -> 215 us  [on_device(): pl.pallas_call(kernel, name='kmeans_step', out_shape=(jax.ShapeDtypeStruc...]
    unnamed x3 -> x0, local copies, waits for them, and re-layouts: 4.4 us -> none
where the time goes in v2:
time: 218 us
  Pallas kernels  217 us (100%)
    pallas_call x1, Pallas kernels, on_device(): pl.pallas_call(kernel, name='kmeans_step', out_shape=(jax.ShapeDtypeStruc...  215 us

profile of v2, /device:TPU:1, one launch (start us, length us, event | category | flops | bytes accessed | tf_op | source)
XLA Modules:
  0.0 217.9 jit_solution(3665603891936638495)
XLA Ops:
  0.6 215.4 %kmeans_step.1 = (f32[48,2048]{1,0:T(8,128)}, f32[1,128]{1,0:T(1,128)}, f32[4,128]{1,0:T(4,128)}, f32[16,1,128]{2,1,0:T(1,128)}) custom-call(bf16[512,2048]{1,0:T(8,128)(2,1)} %data_in.1, bf16[768,2048]{1,0:T(8,128)(2,1)} %cent_in.1, s32[4,16]{1,0:T(4,128)} %bitcast.3), custom_call_target="tpu_custom_call" | custom-call | tf_op jit(solution)/shard_map/kmeans_step/pallas_call | solution.py:564
  216.0 1.8 outputs.1

commit v3 on v2

v3 whole, which is shorter than its diff:
```python
import functools
import math

import jax
import jax.numpy as jnp
from jax import lax
from jax.experimental import pallas as pl
from jax.experimental.pallas import tpu as pltpu
from jax.sharding import PartitionSpec as P

BLOCK = 128
MESH = pl.DeviceIdType.MESH
NEG = -1e30
F32 = jnp.float32
BF16 = jnp.bfloat16


def rcopy(src, dst, ssem, rsem, dev):
    return pltpu.make_async_remote_copy(
        src_ref=src,
        dst_ref=dst,
        send_sem=ssem,
        recv_sem=rsem,
        device_id=dev,
        device_id_type=MESH,
    )


def kernel(
    data_in,
    cent_in,
    mask_in,
    newc,
    shift,
    lognorm,
    peaks,
    data,
    cent,
    mask,
    full,
    got,
    part,
    selb,
    sc,
    wt,
    sums,
    r1,
    r2,
    r3,
    r4,
    te,
    re,
    tot,
    cm,
    cv,
    ct,
    st,
    tops,
    nrm,
    cnorm,
    cacc,
    cbuf,
    csend,
    cret,
    ccol,
    pa,
    load_s,
    code_s,
    code_r,
    cs_s,
    cs_r,
    bc_s,
    bc_r,
    full_s,
    full_r,
    part_s,
    part_r,
    sel_s,
    sel_r,
    stat_s,
    stat_r,
    cnt_s,
    cnt_r,
    r1_s,
    r1_r,
    r2_s,
    r2_r,
    r3_s,
    r3_r,
    r4_s,
    r4_r,
    ret_s,
    ret_r,
    cret_s,
    cret_r,
    pa_s,
    pa_r,
    pb_s,
    pb_r,
):
    half = data.shape[2]
    feat = 2 * half
    width = cent.shape[1]
    own = width // 16
    sharp = 4.0 / math.sqrt(feat)
    p = lax.axis_index("dp")
    m = lax.axis_index("mp")
    z, c = m // 2, lax.rem(m, 2)
    y, x = p // 4, lax.rem(p, 4)
    sign = 1 - 2 * c
    step = (1, -1)
    reach = ((0, 1, -1, 2), (0, 1, -1, -2))
    mine_rows = pl.ds(pl.multiple_of(p * own, own), own)

    def chip(k):
        return lax.rem(z + sign * k + 16, 8)

    def lane(j):
        return c if j == 0 else 1 - c

    def lane_of(j):
        return pl.ds(lane(j), 1)

    def at(k, j):
        return chip(k) * 2 + lane(j)

    def dev(k, j):
        return {"mp": at(k, j)}

    def host(n, k, j):
        if n == 0:
            return at(k, j)
        return at(k + 3, 0) if j == 0 else at(k - 3, 1)

    def slot(n, h, pos, j):
        return got.at[n, h, (pos * 2 + j) * BLOCK : (pos * 2 + j + 1) * BLOCK, :]

    def mp_at(d):
        return lax.rem(m + d, 16)

    def dp_at(d):
        return lax.rem(p + d, 16)

    def each(body):
        lax.fori_loop(1, 16, lambda d, _: (body(d), _)[1], 0)

    barrier = pltpu.get_barrier_semaphore()

    def greet(d):
        pl.semaphore_signal(barrier, inc=1, device_id={"mp": mp_at(d)}, device_id_type=MESH)
        pl.semaphore_signal(barrier, inc=1, device_id={"dp": dp_at(d)}, device_id_type=MESH)

    loads = [pltpu.make_async_copy(mask_in, mask, load_s.at[0])]
    for h in range(2):
        src = data_in.at[:, h * half : (h + 1) * half]
        loads.append(pltpu.make_async_copy(src, data.at[h], load_s.at[1 + h]))
    loads.append(pltpu.make_async_copy(cent_in, cent.at[0], load_s.at[3]))
    for load in loads:
        load.start()
    each(greet)

    loads[0].wait()
    label = (lax.broadcasted_iota(jnp.int32, mask.shape, 0) + 1).astype(F32)
    code = jnp.sum(mask[...].astype(F32) * label, axis=0, keepdims=True)
    cv[m] = code
    shards = lax.broadcasted_iota(jnp.int32, code.shape, 1)
    for n in range(2):
        for j in range(2):
            here = jnp.where(shards == host(n, 0, j), code, 0.0)
            here = jnp.sum(here, axis=1, keepdims=True)
            cm[2 * n + j : 2 * n + j + 1, :] = jnp.broadcast_to(here, (1, BLOCK))
    for load in loads[1:]:
        load.wait()
    pl.semaphore_wait(barrier, 30)

    def code_copy(d):
        return rcopy(cv.at[m], cv.at[m], code_s.at[d], code_r.at[d], {"mp": mp_at(d)})

    def code_wait(d):
        src = lax.rem(m + 16 - d, 16)
        rcopy(cv.at[src], cv.at[src], code_s.at[d], code_r.at[d], {"mp": src}).wait_recv()

    slice_copy = rcopy(cent.at[0, mine_rows], cent.at[1, mine_rows], cs_s.at[0], cs_r.at[0], dev(-3, 0))

    def spread_copy(d):
        ref = cent.at[1, mine_rows]
        return rcopy(ref, ref, bc_s.at[d], bc_r.at[d], {"dp": dp_at(d)})

    def spread_wait(d):
        src = lax.rem(p + 16 - d, 16)
        ref = cent.at[1, pl.ds(pl.multiple_of(src * own, own), own)]
        rcopy(ref, ref, bc_s.at[d], bc_r.at[d], {"dp": src}).wait_recv()

    def full_copy(way, h):
        return rcopy(
            data.at[h], full.at[way, h], full_s.at[way, h], full_r.at[way, h], dev(step[way], 0)
        )

    each(lambda d: code_copy(d).start())
    slice_copy.start()
    for h in range(2):
        for way in range(2):
            full_copy(way, h).start()

    def choose(dst, src, code):
        code = jnp.broadcast_to(code, (BLOCK, BLOCK)).astype(BF16)
        for lanes in range(0, half, BLOCK):
            cols = slice(lanes, lanes + BLOCK)
            out = src[0:BLOCK, cols]
            for b in range(1, src.shape[0] // BLOCK):
                here = code == jnp.asarray(b + 1, BF16)
                out = jnp.where(here, src[b * BLOCK : (b + 1) * BLOCK, cols], out)
            dst[:, cols] = out

    def part_copy(i, n, h):
        return rcopy(
            part.at[i, n, h], slot(n, h, i, 1), part_s.at[i, n, h], part_r.at[i, n, h], dev(0, 1)
        )

    for n in range(2):
        for h in range(2):
            choose(part.at[0, n, h], data.at[h], cm[2 * n + 1 : 2 * n + 2, :])
            choose(slot(n, h, 0, 0), data.at[h], cm[2 * n : 2 * n + 1, :])
    for n in range(2):
        for h in range(2):
            part_copy(0, n, h).start()

    def norms_of(n):
        square = jnp.square(cent[n].astype(F32))
        square = jnp.sum(square, axis=1, keepdims=True)
        cnorm[n] = jnp.broadcast_to(square, cnorm.shape[1:])

    norms_of(0)

    each(code_wait)
    codes = cv[:, 0, :]
    for s in range(16):
        column = jnp.broadcast_to(codes[:, s : s + 1], (16, BLOCK))
        for zg in range(8):
            ct[s, zg] = column[2 * zg : 2 * zg + 2]

    slice_copy.wait_recv()
    each(lambda d: spread_copy(d).start())

    def code_of(k, j, shard):
        return ct[shard, chip(k), lane_of(j), :]

    def product(n, pos, h):
        return lax.dot_general(
            cent[n, :, h * half : (h + 1) * half],
            got[n, h, pos * 256 : (pos + 1) * 256, :],
            (((1,), (1,)), ((), ())),
            preferred_element_type=F32,
        )

    def weigh_up(n, pos, prod):
        score = sharp * (2.0 * prod - cnorm[n, :, 0:1])
        best = jnp.max(score, axis=0, keepdims=True)
        power = jnp.exp(score - best)
        sc[n * 4 + pos] = power.reshape(sc.shape[1:])
        whole = best + jnp.log(jnp.sum(power, axis=0, keepdims=True))
        row = pos * 2 + n
        for j in range(2):
            valid = code_of(reach[n][pos], j, host(n, 0, 0)) > 0.0
            lanes = slice(j * BLOCK, (j + 1) * BLOCK)
            tops[row, lane_of(j), :] = best[:, lanes]
            st[m, row, lane_of(j), :] = jnp.where(valid, whole[:, lanes], NEG)

    def scores(n, pos):
        weigh_up(n, pos, product(n, pos, 0) + product(n, pos, 1))

    def keep(way, h):
        k = -step[way]
        for n in range(2):
            choose(part.at[1 + way, n, h], full.at[way, h], code_of(k, 0, host(n, 0, 1)))
            choose(slot(n, h, 2 - way, 0), full.at[way, h], code_of(k, 0, host(n, 0, 0)))

    def sel_copy(way, j, h):
        n = 1 if way == j else 0
        return rcopy(
            selb.at[way, j, h],
            slot(n, h, 3, j),
            sel_s.at[way, j, h],
            sel_r.at[way, j, h],
            dev(step[way], j),
        )

    def select(way, j, h):
        n = 1 if way == j else 0
        code = code_of(-step[way], 0, host(n, step[way], j))
        choose(selb.at[way, j, h], full.at[way, h], code)

    for h in range(2):
        for way in range(2):
            full_copy(way, h).wait_recv()
            for j in range(2):
                select(way, j, h)
            keep(way, h)
            for j in range(2 - h):
                sel_copy(way, j, h).start()
            for n in range(2):
                part_copy(1 + way, n, h).start()
        if h == 0:
            for hh in range(2):
                part_copy(0, 0, hh).wait_recv()
            scores(0, 0)
    for pos in (1, 2):
        for h in range(2):
            part_copy(pos, 0, h).wait_recv()
        scores(0, pos)
    each(spread_wait)
    norms_of(1)
    for pos in range(3):
        for h in range(2):
            part_copy(pos, 1, h).wait_recv()
        scores(1, pos)

    parts = (slice(0, 6), slice(6, 8))

    def stat_copy(n, d):
        ref = st.at[m, parts[n]]
        return rcopy(ref, ref, stat_s.at[n, d], stat_r.at[n, d], {"mp": mp_at(d)})

    def stat_wait(n, d):
        src = lax.rem(m + 16 - d, 16)
        ref = st.at[src, parts[n]]
        rcopy(ref, ref, stat_s.at[n, d], stat_r.at[n, d], {"mp": src}).wait_recv()

    each(lambda d: stat_copy(0, d).start())
    for way in range(2):
        sel_copy(way, 1, 1).start()
    for h in range(2):
        for way in range(2):
            for j in range(2):
                sel_copy(way, j, h).wait_recv()
        for n in (1, 0):
            prod = product(n, 3, h)
            if h == 0:
                sc[n * 4 + 3] = prod.reshape(sc.shape[1:])
            else:
                weigh_up(n, 3, sc[n * 4 + 3].reshape(width, 256) + prod)
    each(lambda d: stat_copy(1, d).start())
    each(lambda d: stat_wait(0, d))
    each(lambda d: stat_wait(1, d))

    def log_sum(pieces):
        top = functools.reduce(jnp.maximum, pieces)
        ceiling = jnp.maximum(top, 0.0)
        total = functools.reduce(jnp.add, [jnp.exp(piece - ceiling) for piece in pieces])
        return ceiling + jnp.log(jnp.exp(-ceiling) + total)

    near = {0: 0, 1: 1, 7: 2, 2: 3}
    afar = {0: 0, 1: 1, 7: 2, 6: 3}

    def scored(zg, s):
        q, turn = s // 2, 1 - 2 * (s % 2)
        d = (turn * (zg - q)) % 8
        if d in near:
            return s, near[d] * 2
        return ((q - 3 * turn) % 8) * 2 + s % 2, afar[(d + 3) % 8] * 2 + 1

    for zg in range(8):
        for n in range(2):
            mine = ct[host(n, 0, 0), zg]
            pieces = []
            for s in range(16):
                who, row = scored(zg, s)
                pieces.append(jnp.where(ct[s, zg] == mine, st[who, row], NEG))
            nrm[n, zg] = log_sum(pieces)

    def weigh(n):
        for pos in range(4):
            k = reach[n][pos]
            for j in range(2):
                cols = slice(j * BLOCK, (j + 1) * BLOCK)
                gap = tops[pos * 2 + n, lane_of(j), :] - nrm[n, chip(k), lane_of(j), :]
                scale = jnp.where(code_of(k, j, host(n, 0, 0)) > 0.0, jnp.exp(gap), 0.0)
                power = sc[n * 4 + pos, :, :, :, cols].reshape(width, BLOCK)
                weight = power * scale
                if pos == 0 and j == 0:
                    cacc[n] = weight
                else:
                    cacc[n] += weight
                wt[n, :, pos * 256 + j * BLOCK : pos * 256 + (j + 1) * BLOCK] = weight.astype(BF16)

    weigh(1)
    weigh(0)

    each_set = 2 * (half // 256)
    items = 2 * each_set
    held = (sc, sums)
    first = (x, y)
    second = (y, x)

    def dp_dev(a, b):
        return {"dp": lax.rem(y + a + 4, 4) * 4 + lax.rem(x + b + 4, 4)}

    def first_dev(h, d):
        return dp_dev(0, d) if h == 0 else dp_dev(d, 0)

    def second_dev(h, d):
        return dp_dev(d, 0) if h == 0 else dp_dev(0, d)

    def plus(v, d):
        return lax.rem(v + d + 4, 4)

    def item(n):
        i = n % each_set
        return (1 if n < each_set else 0), i, i % 2, i // 2

    def half_rows(way):
        return pl.ds(way * (own // 2), own // 2)

    def copy1(n, way):
        e, i, h, q = item(n)
        src = held[e].at[i, plus(first[h], 2), 2 * way : 2 * way + 2]
        return rcopy(src, r1.at[n, way], r1_s.at[n, way], r1_r.at[n, way], first_dev(h, step[way]))

    def copy2(n, way):
        e, i, h, q = item(n)
        src = held[e].at[i, plus(first[h], step[way])]
        return rcopy(src, r2.at[n, way], r2_s.at[n, way], r2_r.at[n, way], first_dev(h, step[way]))

    def copy3(n, way):
        e, i, h, q = item(n)
        src = held[e].at[i, first[h], plus(second[h], 2), half_rows(way)]
        return rcopy(src, r3.at[n, way], r3_s.at[n, way], r3_r.at[n, way], second_dev(h, step[way]))

    def copy4(n, way):
        e, i, h, q = item(n)
        src = held[e].at[i, first[h], plus(second[h], step[way])]
        return rcopy(src, r4.at[n, way], r4_s.at[n, way], r4_r.at[n, way], second_dev(h, step[way]))

    def back_copy(i):
        return rcopy(te.at[i], re.at[i], ret_s.at[i], ret_r.at[i], dev(3, 0))

    def stage1(n):
        e, i, h, q = item(n)
        out = jnp.dot(wt[e], got[e, h, :, q * 256 : (q + 1) * 256], preferred_element_type=F32)
        for owner in range(16):
            yy, xx = owner // 4, owner % 4
            a, b = (xx, yy) if h == 0 else (yy, xx)
            held[e][i, a, b] = out[owner * own : (owner + 1) * own]
        for way in range(2):
            copy1(n, way).start()

    def stage2(n):
        e, i, h, q = item(n)
        for way in range(2):
            copy1(n, way).wait_recv()
            a = plus(first[h], step[way])
            held[e][i, a, 2 * way : 2 * way + 2] += r1[n, way]
            copy2(n, way).start()

    def stage3(n):
        e, i, h, q = item(n)
        for way in range(2):
            copy2(n, way).wait_recv()
        held[e][i, first[h]] += r2[n, 0] + r2[n, 1]
        for way in range(2):
            copy3(n, way).start()

    def stage4(n):
        e, i, h, q = item(n)
        for way in range(2):
            copy3(n, way).wait_recv()
            held[e][i, first[h], plus(second[h], step[way]), half_rows(way)] += r3[n, way]
            copy4(n, way).start()

    def finish(n):
        e, i, h, q = item(n)
        for way in range(2):
            copy4(n, way).wait_recv()
        value = held[e][i, first[h], second[h]] + r4[n, 0] + r4[n, 1]
        if e == 1:
            te[i] = value
            back_copy(i).start()
        else:
            back_copy(i).wait_recv()
            cols = slice(h * half + q * 256, h * half + (q + 1) * 256)
            tot[:, cols] = value + re[i]

    def cnt_copy(d):
        return rcopy(cbuf.at[p], cbuf.at[p], cnt_s.at[d], cnt_r.at[d], {"dp": dp_at(d)})

    def cnt_wait(d):
        src = lax.rem(p + 16 - d, 16)
        rcopy(cbuf.at[src], cbuf.at[src], cnt_s.at[d], cnt_r.at[d], {"dp": src}).wait_recv()

    count_back = rcopy(csend, cret, cret_s.at[0], cret_r.at[0], dev(3, 0))

    stages = ((stage1, 0), (stage2, 3), (stage3, 8), (stage4, 13), (finish, 18))
    for t in range(items + 18):
        for stage, late in stages:
            if 0 <= t - late < items:
                stage(t - late)
        if t == 3:
            for n in range(2):
                cbuf[p, n] = jnp.sum(cacc[n].T, axis=0, keepdims=True)
            each(lambda d: cnt_copy(d).start())
        if t == items - 1:
            each(cnt_wait)
            csend[...] = jnp.sum(cbuf[:, 1], axis=0)
            count_back.start()
            number = (lax.broadcasted_iota(jnp.int32, (4, BLOCK), 0) + 1).astype(F32)
            pieces = []
            for s in range(16):
                q, turn = s // 2, 1 - 2 * (s % 2)
                d = lax.rem(turn * (z - q) + 16, 8)
                at_home = (d <= 2) | (d == 7)
                who = jnp.where(at_home, s, lax.rem(q - 3 * turn + 8, 8) * 2 + s % 2)
                d = jnp.where(at_home, d, lax.rem(d + 3, 8))
                pos = jnp.where(d == 0, 0, jnp.where(d == 1, 1, jnp.where(d == 7, 2, 3)))
                row = pos * 2 + jnp.where(at_home, 0, 1)
                here = ct[s, z, lane_of(0), :] == number
                pieces.append(jnp.where(here, st[who, row, lane_of(0), :], NEG))
            lognorm[...] = log_sum(pieces)
        if t == items + 4:
            count_back.wait_recv()
            count = jnp.sum(cbuf[:, 0], axis=0) + cret[...]
            ccol[...] = jnp.broadcast_to(count, (BLOCK, width)).T

    old = cent[0, mine_rows, :].astype(F32)
    denom = ccol[mine_rows, 0:1] + 1.0
    updated = (tot[...] + old) / denom
    newc[...] = updated
    move = jnp.sqrt(jnp.sum(jnp.square(updated - old), axis=1, keepdims=True) + 1.0)
    wide = jnp.broadcast_to(move, (own, BLOCK))
    pa[p] = jnp.max(wide, axis=0, keepdims=True)

    def pa_copy(d):
        return rcopy(pa.at[p], pa.at[p], pa_s.at[d], pa_r.at[d], {"dp": dp_at(d)})

    def pa_wait(d):
        src = lax.rem(p + 16 - d, 16)
        rcopy(pa.at[src], pa.at[src], pa_s.at[d], pa_r.at[d], {"dp": src}).wait_recv()

    each(lambda d: pa_copy(d).start())
    tall = jnp.concatenate([wide, jnp.zeros((BLOCK - own, BLOCK), F32)], axis=0)
    shift[...] = tall.T[0:1, :]

    slice_copy.wait_send()
    count_back.wait_send()
    for h in range(2):
        for way in range(2):
            full_copy(way, h).wait_send()
            for j in range(2):
                sel_copy(way, j, h).wait_send()
        for n in range(2):
            for i in range(3):
                part_copy(i, n, h).wait_send()
    for n in range(items):
        for way in range(2):
            for copy in (copy1, copy2, copy3, copy4):
                copy(n, way).wait_send()
    for i in range(each_set):
        back_copy(i).wait_send()

    def sent(d):
        for copy in (code_copy, spread_copy, cnt_copy):
            copy(d).wait_send()
        for n in range(2):
            stat_copy(n, d).wait_send()

    each(sent)

    each(pa_wait)
    peaks[m] = jnp.max(pa[...], axis=0)

    def pb_copy(d):
        return rcopy(peaks.at[m], peaks.at[m], pb_s.at[d], pb_r.at[d], {"mp": mp_at(d)})

    def pb_wait(d):
        src = lax.rem(m + 16 - d, 16)
        rcopy(peaks.at[src], peaks.at[src], pb_s.at[d], pb_r.at[d], {"mp": src}).wait_recv()

    each(lambda d: pb_copy(d).start())
    each(lambda d: pa_copy(d).wait_send())
    each(pb_wait)
    each(lambda d: pb_copy(d).wait_send())


def outputs(made, width, logs, peaks, lower, newc, shift, lognorm, newlow):
    newc[...] = made[...]
    shift[...] = width[:, : shift.shape[1]]
    lognorm[...] = logs[...]
    for s in range(16):
        newlow[s : s + 1, :] = lower[s : s + 1, :] - jnp.concatenate([peaks[s]] * 4, axis=1)


def on_device(data_rows, centroids, block_mask, lower_bound):
    rows, feat = data_rows.shape
    blocks = rows // BLOCK
    width = centroids.shape[0]
    half = feat // 2
    own = width // 16
    items = 2 * (feat // 256)
    dma = pltpu.SemaphoreType.DMA
    vmem = pltpu.VMEM
    made, movement, log_norm, peaks = pl.pallas_call(
        kernel,
        name="kmeans_step",
        out_shape=(
            jax.ShapeDtypeStruct((own, feat), F32),
            jax.ShapeDtypeStruct((1, BLOCK), F32),
            jax.ShapeDtypeStruct((blocks, BLOCK), F32),
            jax.ShapeDtypeStruct((16, 1, BLOCK), F32),
        ),
        in_specs=[pl.BlockSpec(memory_space=pl.ANY)] * 3,
        out_specs=[pl.BlockSpec(memory_space=vmem)] * 4,
        scratch_shapes=[
            vmem((2, rows, half), BF16),
            vmem((2, width, feat), BF16),
            vmem((blocks, 16), jnp.int32),
            vmem((2, 2, rows, half), BF16),
            vmem((2, 2, 8 * BLOCK, half), BF16),
            vmem((3, 2, 2, BLOCK, half), BF16),
            vmem((2, 2, 2, BLOCK, half), BF16),
            vmem((8, 4, 4, own, 256), F32),
            vmem((2, width, 8 * BLOCK), BF16),
            vmem((8, 4, 4, own, 256), F32),
            vmem((items, 2, 2, own, 256), F32),
            vmem((items, 2, 4, own, 256), F32),
            vmem((items, 2, own // 2, 256), F32),
            vmem((items, 2, own, 256), F32),
            vmem((8, own, 256), F32),
            vmem((8, own, 256), F32),
            vmem((own, feat), F32),
            vmem((4, BLOCK), F32),
            vmem((16, 1, 16), F32),
            vmem((16, 8, 2, BLOCK), F32),
            vmem((16, 8, 2, BLOCK), F32),
            vmem((8, 2, BLOCK), F32),
            vmem((2, 8, 2, BLOCK), F32),
            vmem((2, width, BLOCK), F32),
            vmem((2, width, BLOCK), F32),
            vmem((16, 2, 1, width), F32),
            vmem((1, width), F32),
            vmem((1, width), F32),
            vmem((width, BLOCK), F32),
            vmem((16, 1, BLOCK), F32),
            dma((4,)),
            dma((16,)),
            dma((16,)),
            dma((1,)),
            dma((1,)),
            dma((16,)),
            dma((16,)),
            dma((2, 2)),
            dma((2, 2)),
            dma((3, 2, 2)),
            dma((3, 2, 2)),
            dma((2, 2, 2)),
            dma((2, 2, 2)),
            dma((2, 16)),
            dma((2, 16)),
            dma((16,)),
            dma((16,)),
            *[dma((items, 2)) for _ in range(8)],
            dma((8,)),
            dma((8,)),
            dma((1,)),
            dma((1,)),
            *[dma((16,)) for _ in range(4)],
        ],
        compiler_params=pltpu.CompilerParams(
            collective_id=0, has_side_effects=True, vmem_limit_bytes=66_000_000
        ),
    )(data_rows, centroids, block_mask.T)
    updated, movement, log_norm, new_lower = pl.pallas_call(
        outputs,
        name="outputs",
        out_shape=(
            jax.ShapeDtypeStruct(made.shape, F32),
            jax.ShapeDtypeStruct((1, own), F32),
            jax.ShapeDtypeStruct(log_norm.shape, F32),
            jax.ShapeDtypeStruct(lower_bound.shape, F32),
        ),
        in_specs=[pl.BlockSpec(memory_space=vmem)] * 5,
        out_specs=[pl.BlockSpec(memory_space=vmem)] * 4,
    )(made, movement, log_norm, peaks, lower_bound)
    return updated, movement.reshape(-1), log_norm.reshape(-1), new_lower


def solution(mesh):
    in_specs = (
        P(("dp", "mp"), None),
        P("mp", None),
        P(None, ("dp", "mp")),
        P(None, ("dp", "mp")),
    )
    out_specs = (
        P(("mp", "dp"), None),
        P(("mp", "dp")),
        P(("dp", "mp")),
        P(None, ("dp", "mp")),
    )
    return jax.shard_map(
        on_device, mesh=mesh, in_specs=in_specs, out_specs=out_specs, check_vma=False
    )
```

time: 218 us -> 187 us (0.86)
  Pallas kernels: 217 us -> 186 us
    pallas_call x1, Pallas kernels: 215 us -> 184 us  [on_device(): pl.pallas_call(kernel, name='kmeans_step', out_shape=(jax.ShapeDtypeStruc...]
where the time goes in v3:
time: 187 us
  Pallas kernels  186 us (99%)
    pallas_call x1, Pallas kernels, on_device(): pl.pallas_call(kernel, name='kmeans_step', out_shape=(jax.ShapeDtypeStruc...  184 us

profile of v3, /device:TPU:1, one launch (start us, length us, event | category | flops | bytes accessed | tf_op | source)
XLA Modules:
  0.0 186.9 jit_solution(15351070616076075574)
XLA Ops:
  0.6 184.5 %kmeans_step.1 = (f32[48,2048]{1,0:T(8,128)}, f32[1,128]{1,0:T(1,128)}, f32[4,128]{1,0:T(4,128)}, f32[16,1,128]{2,1,0:T(1,128)}) custom-call(bf16[512,2048]{1,0:T(8,128)(2,1)} %data_in.1, bf16[768,2048]{1,0:T(8,128)(2,1)} %cent_in.1, s32[4,16]{1,0:T(4,128)} %bitcast.3), custom_call_target="tpu_custom_call" | custom-call | tf_op jit(solution)/shard_map/kmeans_step/pallas_call | solution.py:600
  185.1 1.8 outputs.1

commit v4 on v3

--- a/solution.py
+++ b/solution.py
@@ -44,6 +44,7 @@
     sc,
     wt,
     sums,
+    s1,
     r1,
     r2,
     r3,
@@ -412,9 +413,8 @@
         return pl.ds(way * (own // 2), own // 2)
 
     def copy1(n, way):
-        e, i, h, q = item(n)
-        src = held[e].at[i, plus(first[h], 2), 2 * way : 2 * way + 2]
-        return rcopy(src, r1.at[n, way], r1_s.at[n, way], r1_r.at[n, way], first_dev(h, step[way]))
+        h = item(n)[2]
+        return rcopy(s1.at[n, way], r1.at[n, way], r1_s.at[n, way], r1_r.at[n, way], first_dev(h, step[way]))
 
     def copy2(n, way):
         e, i, h, q = item(n)
@@ -442,6 +442,8 @@
             a, b = (xx, yy) if h == 0 else (yy, xx)
             held[e][i, a, b] = out[owner * own : (owner + 1) * own]
         for way in range(2):
+            s1[n, way] = held[e][i, plus(first[h], 2), 2 * way : 2 * way + 2].astype(BF16)
+        for way in range(2):
             copy1(n, way).start()
 
     def stage2(n):
@@ -449,7 +451,7 @@
         for way in range(2):
             copy1(n, way).wait_recv()
             a = plus(first[h], step[way])
-            held[e][i, a, 2 * way : 2 * way + 2] += r1[n, way]
+            held[e][i, a, 2 * way : 2 * way + 2] += r1[n, way].astype(F32)
             copy2(n, way).start()
 
     def stage3(n):
@@ -619,7 +621,8 @@
             vmem((8, 4, 4, own, 256), F32),
             vmem((2, width, 8 * BLOCK), BF16),
             vmem((8, 4, 4, own, 256), F32),
-            vmem((items, 2, 2, own, 256), F32),
+            vmem((items, 2, 2, own, 256), BF16),
+            vmem((items, 2, 2, own, 256), BF16),
             vmem((items, 2, 4, own, 256), F32),
             vmem((items, 2, own // 2, 256), F32),
             vmem((items, 2, own, 256), F32),

time: 187 us -> 180 us (0.963)
  Pallas kernels: 186 us -> 179 us
    pallas_call x1, Pallas kernels: 184 us -> 177 us  [on_device(): pl.pallas_call(kernel, name='kmeans_step', out_shape=(jax.ShapeDtypeStruc...]
where the time goes in v4:
time: 180 us; the launch traced here: 179 us
  Pallas kernels  179 us (99%)
    pallas_call x1, Pallas kernels, on_device(): pl.pallas_call(kernel, name='kmeans_step', out_shape=(jax.ShapeDtypeStruc...  177 us

profile of v4, /device:TPU:1, one launch (start us, length us, event | category | flops | bytes accessed | tf_op | source)
XLA Modules:
  0.0 179.5 jit_solution(13691980617552106797)
XLA Ops:
  0.6 177.0 %kmeans_step.1 = (f32[48,2048]{1,0:T(8,128)}, f32[1,128]{1,0:T(1,128)}, f32[4,128]{1,0:T(4,128)}, f32[16,1,128]{2,1,0:T(1,128)}) custom-call(bf16[512,2048]{1,0:T(8,128)(2,1)} %data_in.1, bf16[768,2048]{1,0:T(8,128)(2,1)} %cent_in.1, s32[4,16]{1,0:T(4,128)} %bitcast.3), custom_call_target="tpu_custom_call" | custom-call | tf_op jit(solution)/shard_map/kmeans_step/pallas_call | solution.py:602
  177.7 1.8 %outputs.1 = (f32[48,2048]{1,0:T(8,128)}, f32[1,48]{1,0:T(1,128)}, f32[4,128]{1,0:T(4,128)}, f32[16,512]{1,0:T(8,128)}) custom-call(f32[48,2048]{1,0:T(8,128)} %get-tuple-element.12.made, f32[1,128]{1,0:T(1,128)} %get-tuple-element.13.width, f32[4,128]{1,0:T(4,128)} %get-tuple-element.14.logs, f32[16,1,128]{2,1,0:T(1,128)} %get-tuple-element.15.peaks, ...), custom_call_target="tpu_custom_call" | custom-call | tf_op jit(solution)/shard_map/outputs/pallas_call | solution.py:673

commit v5 on v4

--- a/solution.py
+++ b/solution.py
@@ -51,6 +51,7 @@
     r4,
     te,
     re,
+    rz,
     tot,
     cm,
     cv,
@@ -90,10 +91,14 @@
     r3_r,
     r4_s,
     r4_r,
+    r5_s,
+    r5_r,
     ret_s,
     ret_r,
     cret_s,
     cret_r,
+    rz_s,
+    rz_r,
     pa_s,
     pa_r,
     pb_s,
@@ -297,7 +302,7 @@
             for j in range(2):
                 select(way, j, h)
             keep(way, h)
-            for j in range(2 - h):
+            for j in (way, 1 - way)[: 2 - h]:
                 sel_copy(way, j, h).start()
             for n in range(2):
                 part_copy(1 + way, n, h).start()
@@ -329,12 +334,11 @@
 
     each(lambda d: stat_copy(0, d).start())
     for way in range(2):
-        sel_copy(way, 1, 1).start()
+        sel_copy(way, 1 - way, 1).start()
     for h in range(2):
-        for way in range(2):
-            for j in range(2):
-                sel_copy(way, j, h).wait_recv()
         for n in (1, 0):
+            for way in range(2):
+                sel_copy(way, way if n == 1 else 1 - way, h).wait_recv()
             prod = product(n, 3, h)
             if h == 0:
                 sc[n * 4 + 3] = prod.reshape(sc.shape[1:])
@@ -385,7 +389,6 @@
                 wt[n, :, pos * 256 + j * BLOCK : pos * 256 + (j + 1) * BLOCK] = weight.astype(BF16)
 
     weigh(1)
-    weigh(0)
 
     each_set = 2 * (half // 256)
     items = 2 * each_set
@@ -405,34 +408,58 @@
     def plus(v, d):
         return lax.rem(v + d + 4, 4)
 
+    last_q = half // 256 - 1
+
     def item(n):
         i = n % each_set
-        return (1 if n < each_set else 0), i, i % 2, i // 2
+        h, q = i % 2, i // 2
+        if n < each_set:
+            q = (q + last_q) % (last_q + 1)
+        return (1 if n < each_set else 0), 2 * q + h, h, q
 
     def half_rows(way):
         return pl.ds(way * (own // 2), own // 2)
 
+    def wide(n):
+        return pl.ds(0, BLOCK if n < 2 else 256)
+
+    def direct(n):
+        return n >= items - 2
+
     def copy1(n, way):
-        h = item(n)[2]
-        return rcopy(s1.at[n, way], r1.at[n, way], r1_s.at[n, way], r1_r.at[n, way], first_dev(h, step[way]))
-
-    def copy2(n, way):
-        e, i, h, q = item(n)
-        src = held[e].at[i, plus(first[h], step[way])]
-        return rcopy(src, r2.at[n, way], r2_s.at[n, way], r2_r.at[n, way], first_dev(h, step[way]))
+        h, cols = item(n)[2], wide(n)
+        src, dst = s1.at[n, way, :, :, cols], r1.at[n, way, :, :, cols]
+        return rcopy(src, dst, r1_s.at[n, way], r1_r.at[n, way], first_dev(h, step[way]))
+
+    def copy2(n, way, late):
+        (e, i, h, q), cols = item(n), wide(n)
+        some = slice(0, 2) if late == (way == 0) else slice(2, 4)
+        src = held[e].at[i, plus(first[h], step[way]), some, :, cols]
+        dst = r2.at[n, way, some, :, cols]
+        sems = (r2_s, r2_r) if late else (r5_s, r5_r)
+        return rcopy(src, dst, sems[0].at[n, way], sems[1].at[n, way], first_dev(h, step[way]))
 
     def copy3(n, way):
-        e, i, h, q = item(n)
-        src = held[e].at[i, first[h], plus(second[h], 2), half_rows(way)]
-        return rcopy(src, r3.at[n, way], r3_s.at[n, way], r3_r.at[n, way], second_dev(h, step[way]))
+        (e, i, h, q), cols = item(n), wide(n)
+        src = held[e].at[i, first[h], plus(second[h], 2), half_rows(way), cols]
+        dst = r3.at[n, way, :, cols]
+        hops = 2 if direct(n) else step[way]
+        return rcopy(src, dst, r3_s.at[n, way], r3_r.at[n, way], second_dev(h, hops))
 
     def copy4(n, way):
-        e, i, h, q = item(n)
-        src = held[e].at[i, first[h], plus(second[h], step[way])]
-        return rcopy(src, r4.at[n, way], r4_s.at[n, way], r4_r.at[n, way], second_dev(h, step[way]))
+        (e, i, h, q), cols = item(n), wide(n)
+        src = held[e].at[i, first[h], plus(second[h], step[way]), :, cols]
+        dst = r4.at[n, way, :, cols]
+        return rcopy(src, dst, r4_s.at[n, way], r4_r.at[n, way], second_dev(h, step[way]))
 
     def back_copy(i):
-        return rcopy(te.at[i], re.at[i], ret_s.at[i], ret_r.at[i], dev(3, 0))
+        cols = wide(0 if i // 2 == last_q else items)
+        src, dst = te.at[i, :, cols], re.at[i, :, cols]
+        return rcopy(src, dst, ret_s.at[i], ret_r.at[i], dev(3, 0))
+
+    def home_copy(h):
+        src = sums.at[2 * last_q + h, :, :, :, BLOCK:256]
+        return rcopy(src, rz.at[h], rz_s.at[h], rz_r.at[h], dev(3, 0))
 
     def stage1(n):
         e, i, h, q = item(n)
@@ -441,46 +468,66 @@
             yy, xx = owner // 4, owner % 4
             a, b = (xx, yy) if h == 0 else (yy, xx)
             held[e][i, a, b] = out[owner * own : (owner + 1) * own]
+        if n >= items - 2:
+            home_copy(h).wait_recv()
+            held[e][i, :, :, :, BLOCK:256] += rz[h]
         for way in range(2):
             s1[n, way] = held[e][i, plus(first[h], 2), 2 * way : 2 * way + 2].astype(BF16)
         for way in range(2):
             copy1(n, way).start()
+        for way in range(2):
+            copy2(n, way, False).start()
+        if n < 2:
+            home_copy(h).start()
 
     def stage2(n):
-        e, i, h, q = item(n)
+        (e, i, h, q), cols = item(n), wide(n)
         for way in range(2):
             copy1(n, way).wait_recv()
             a = plus(first[h], step[way])
-            held[e][i, a, 2 * way : 2 * way + 2] += r1[n, way].astype(F32)
-            copy2(n, way).start()
+            held[e][i, a, 2 * way : 2 * way + 2, :, cols] += r1[n, way, :, :, cols].astype(F32)
+            copy2(n, way, True).start()
 
     def stage3(n):
-        e, i, h, q = item(n)
-        for way in range(2):
-            copy2(n, way).wait_recv()
-        held[e][i, first[h]] += r2[n, 0] + r2[n, 1]
+        (e, i, h, q), cols = item(n), wide(n)
+        for way in range(2):
+            copy2(n, way, False).wait_recv()
+            copy2(n, way, True).wait_recv()
+        held[e][i, first[h], :, :, cols] += r2[n, 0, :, :, cols] + r2[n, 1, :, :, cols]
         for way in range(2):
             copy3(n, way).start()
+        if direct(n):
+            for way in range(2):
+                copy4(n, way).start()
 
     def stage4(n):
-        e, i, h, q = item(n)
+        if direct(n):
+            return
+        (e, i, h, q), cols = item(n), wide(n)
         for way in range(2):
             copy3(n, way).wait_recv()
-            held[e][i, first[h], plus(second[h], step[way]), half_rows(way)] += r3[n, way]
+            b = plus(second[h], step[way])
+            held[e][i, first[h], b, half_rows(way), cols] += r3[n, way, :, cols]
             copy4(n, way).start()
 
     def finish(n):
-        e, i, h, q = item(n)
+        (e, i, h, q), cols = item(n), wide(n)
         for way in range(2):
             copy4(n, way).wait_recv()
-        value = held[e][i, first[h], second[h]] + r4[n, 0] + r4[n, 1]
+            if direct(n):
+                copy3(n, way).wait_recv()
+        value = held[e][i, first[h], second[h], :, cols] + r4[n, 0, :, cols] + r4[n, 1, :, cols]
+        if direct(n):
+            value = value + jnp.concatenate([r3[n, 0], r3[n, 1]], axis=0)
         if e == 1:
-            te[i] = value
+            te[i, :, cols] = value
             back_copy(i).start()
         else:
             back_copy(i).wait_recv()
-            cols = slice(h * half + q * 256, h * half + (q + 1) * 256)
-            tot[:, cols] = value + re[i]
+            start = h * half + q * 256
+            tot[:, start : start + 256] = value
+            had = BLOCK if q == last_q else 256
+            tot[:, start : start + had] += re[i, :, :had]
 
     def cnt_copy(d):
         return rcopy(cbuf.at[p], cbuf.at[p], cnt_s.at[d], cnt_r.at[d], {"dp": dp_at(d)})
@@ -497,6 +544,7 @@
             if 0 <= t - late < items:
                 stage(t - late)
         if t == 3:
+            weigh(0)
             for n in range(2):
                 cbuf[p, n] = jnp.sum(cacc[n].T, axis=0, keepdims=True)
             each(lambda d: cnt_copy(d).start())
@@ -527,8 +575,8 @@
     updated = (tot[...] + old) / denom
     newc[...] = updated
     move = jnp.sqrt(jnp.sum(jnp.square(updated - old), axis=1, keepdims=True) + 1.0)
-    wide = jnp.broadcast_to(move, (own, BLOCK))
-    pa[p] = jnp.max(wide, axis=0, keepdims=True)
+    moves = jnp.broadcast_to(move, (own, BLOCK))
+    pa[p] = jnp.max(moves, axis=0, keepdims=True)
 
     def pa_copy(d):
         return rcopy(pa.at[p], pa.at[p], pa_s.at[d], pa_r.at[d], {"dp": dp_at(d)})
@@ -538,7 +586,7 @@
         rcopy(pa.at[src], pa.at[src], pa_s.at[d], pa_r.at[d], {"dp": src}).wait_recv()
 
     each(lambda d: pa_copy(d).start())
-    tall = jnp.concatenate([wide, jnp.zeros((BLOCK - own, BLOCK), F32)], axis=0)
+    tall = jnp.concatenate([moves, jnp.zeros((BLOCK - own, BLOCK), F32)], axis=0)
     shift[...] = tall.T[0:1, :]
 
     slice_copy.wait_send()
@@ -553,10 +601,14 @@
                 part_copy(i, n, h).wait_send()
     for n in range(items):
         for way in range(2):
-            for copy in (copy1, copy2, copy3, copy4):
+            for copy in (copy1, copy3, copy4):
                 copy(n, way).wait_send()
+            for late in (False, True):
+                copy2(n, way, late).wait_send()
     for i in range(each_set):
         back_copy(i).wait_send()
+    for h in range(2):
+        home_copy(h).wait_send()
 
     def sent(d):
         for copy in (code_copy, spread_copy, cnt_copy):
@@ -628,6 +680,7 @@
             vmem((items, 2, own, 256), F32),
             vmem((8, own, 256), F32),
             vmem((8, own, 256), F32),
+            vmem((2, 4, 4, own, BLOCK), F32),
             vmem((own, feat), F32),
             vmem((4, BLOCK), F32),
             vmem((16, 1, 16), F32),
@@ -659,11 +712,13 @@
             dma((2, 16)),
             dma((16,)),
             dma((16,)),
-            *[dma((items, 2)) for _ in range(8)],
+            *[dma((items, 2)) for _ in range(10)],
             dma((8,)),
             dma((8,)),
             dma((1,)),
             dma((1,)),
+            dma((2,)),
+            dma((2,)),
             *[dma((16,)) for _ in range(4)],
         ],
         compiler_params=pltpu.CompilerParams(

time: 180 us -> 174 us (0.967)
  Pallas kernels: 179 us -> 174 us
    pallas_call x1, Pallas kernels: 177 us -> 172 us  [on_device(): pl.pallas_call(kernel, name='kmeans_step', out_shape=(jax.ShapeDtypeStruc...]
where the time goes in v5:
time: 174 us
  Pallas kernels  174 us (100%)
    pallas_call x1, Pallas kernels, on_device(): pl.pallas_call(kernel, name='kmeans_step', out_shape=(jax.ShapeDtypeStruc...  172 us

profile of v5, /device:TPU:1, one launch (start us, length us, event | category | flops | bytes accessed | tf_op | source)
XLA Modules:
  0.0 174.2 jit_solution(15415770499272572411)
XLA Ops:
  0.6 171.7 %kmeans_step.1 = (f32[48,2048]{1,0:T(8,128)}, f32[1,128]{1,0:T(1,128)}, f32[4,128]{1,0:T(4,128)}, f32[16,1,128]{2,1,0:T(1,128)}) custom-call(bf16[512,2048]{1,0:T(8,128)(2,1)} %data_in.1, bf16[768,2048]{1,0:T(8,128)(2,1)} %cent_in.1, s32[4,16]{1,0:T(4,128)} %bitcast.3), custom_call_target="tpu_custom_call" | custom-call | tf_op jit(solution)/shard_map/kmeans_step/pallas_call | solution.py:654
  172.4 1.8 %outputs.1 = (f32[48,2048]{1,0:T(8,128)}, f32[1,48]{1,0:T(1,128)}, f32[4,128]{1,0:T(4,128)}, f32[16,512]{1,0:T(8,128)}) custom-call(f32[48,2048]{1,0:T(8,128)} %get-tuple-element.12.made, f32[1,128]{1,0:T(1,128)} %get-tuple-element.13.width, f32[4,128]{1,0:T(4,128)} %get-tuple-element.14.logs, f32[16,1,128]{2,1,0:T(1,128)} %get-tuple-element.15.peaks, ...), custom_call_target="tpu_custom_call" | custom-call | tf_op jit(solution)/shard_map/outputs/pallas_call | solution.py:728

commit v6 on v5

--- a/solution.py
+++ b/solution.py
@@ -251,6 +251,9 @@
     def code_of(k, j, shard):
         return ct[shard, chip(k), lane_of(j), :]
 
+    def row_of(pos, n):
+        return (1, 0, 2, 3)[pos] * 2 + n
+
     def product(n, pos, h):
         return lax.dot_general(
             cent[n, :, h * half : (h + 1) * half],
@@ -265,7 +268,7 @@
         power = jnp.exp(score - best)
         sc[n * 4 + pos] = power.reshape(sc.shape[1:])
         whole = best + jnp.log(jnp.sum(power, axis=0, keepdims=True))
-        row = pos * 2 + n
+        row = row_of(pos, n)
         for j in range(2):
             valid = code_of(reach[n][pos], j, host(n, 0, 0)) > 0.0
             lanes = slice(j * BLOCK, (j + 1) * BLOCK)
@@ -321,18 +324,21 @@
             part_copy(pos, 1, h).wait_recv()
         scores(1, pos)
 
-    parts = (slice(0, 6), slice(6, 8))
-
-    def stat_copy(n, d):
-        ref = st.at[m, parts[n]]
-        return rcopy(ref, ref, stat_s.at[n, d], stat_r.at[n, d], {"mp": mp_at(d)})
-
-    def stat_wait(n, d):
-        src = lax.rem(m + 16 - d, 16)
-        ref = st.at[src, parts[n]]
-        rcopy(ref, ref, stat_s.at[n, d], stat_r.at[n, d], {"mp": src}).wait_recv()
-
-    each(lambda d: stat_copy(0, d).start())
+    early = {0: (0, 6), 1: (0, 6), -1: (0, 6), 2: (0, 4), -2: (2, 6), 3: (0, 2), -3: (4, 6)}
+    final = {k: (6 if k >= 0 else 7, 7 if 0 < k < 4 else 8) for k in range(-3, 5)}
+    peers = [(k, j) for k in range(-3, 5) for j in range(2) if (k, j) != (0, 0)]
+
+    def stat_copy(n, k, j, came):
+        rows = (early, final)[n][k]
+        src = m if not came else at(-k, 0) if j == 0 else at(k, 1)
+        ref, i = st.at[src, rows[0] : rows[1]], (k + 3) * 2 + j
+        return rcopy(ref, ref, stat_s.at[n, i], stat_r.at[n, i], {"mp": src} if came else dev(k, j))
+
+    def stats(n):
+        return [(n, k, j) for k, j in peers if n == 1 or k < 4]
+
+    for one in stats(0):
+        stat_copy(*one, False).start()
     for way in range(2):
         sel_copy(way, 1 - way, 1).start()
     for h in range(2):
@@ -344,9 +350,10 @@
                 sc[n * 4 + 3] = prod.reshape(sc.shape[1:])
             else:
                 weigh_up(n, 3, sc[n * 4 + 3].reshape(width, 256) + prod)
-    each(lambda d: stat_copy(1, d).start())
-    each(lambda d: stat_wait(0, d))
-    each(lambda d: stat_wait(1, d))
+    for one in stats(1):
+        stat_copy(*one, False).start()
+    for one in stats(0) + stats(1):
+        stat_copy(*one, True).wait_recv()
 
     def log_sum(pieces):
         top = functools.reduce(jnp.maximum, pieces)
@@ -357,28 +364,32 @@
     near = {0: 0, 1: 1, 7: 2, 2: 3}
     afar = {0: 0, 1: 1, 7: 2, 6: 3}
 
-    def scored(zg, s):
-        q, turn = s // 2, 1 - 2 * (s % 2)
-        d = (turn * (zg - q)) % 8
-        if d in near:
-            return s, near[d] * 2
-        return ((q - 3 * turn) % 8) * 2 + s % 2, afar[(d + 3) % 8] * 2 + 1
-
-    for zg in range(8):
-        for n in range(2):
-            mine = ct[host(n, 0, 0), zg]
-            pieces = []
-            for s in range(16):
-                who, row = scored(zg, s)
-                pieces.append(jnp.where(ct[s, zg] == mine, st[who, row], NEG))
-            nrm[n, zg] = log_sum(pieces)
+    def log_sums(k, mine, lanes):
+        pieces = []
+        for q in range(-3, 5):
+            for j in range(2):
+                turn = 1 - 2 * j
+                d = turn * (k - q) % 8
+                who, row = at(q, j), 0
+                if d in near:
+                    row = row_of(near[d], 0)
+                else:
+                    who, row = at(q - 3 * turn, j), row_of(afar[(d + 3) % 8], 1)
+                here = ct[at(q, j), chip(k), lanes, :] == mine
+                pieces.append(jnp.where(here, st[who, row, lanes, :], NEG))
+        return log_sum(pieces)
+
+    for n in range(2):
+        for pos in range(4):
+            k = reach[n][pos]
+            nrm[n, pos] = log_sums(k, ct[host(n, 0, 0), chip(k)], slice(0, 2))
 
     def weigh(n):
         for pos in range(4):
             k = reach[n][pos]
             for j in range(2):
                 cols = slice(j * BLOCK, (j + 1) * BLOCK)
-                gap = tops[pos * 2 + n, lane_of(j), :] - nrm[n, chip(k), lane_of(j), :]
+                gap = tops[row_of(pos, n), lane_of(j), :] - nrm[n, pos, lane_of(j), :]
                 scale = jnp.where(code_of(k, j, host(n, 0, 0)) > 0.0, jnp.exp(gap), 0.0)
                 power = sc[n * 4 + pos, :, :, :, cols].reshape(width, BLOCK)
                 weight = power * scale
@@ -538,8 +549,8 @@
 
     count_back = rcopy(csend, cret, cret_s.at[0], cret_r.at[0], dev(3, 0))
 
-    stages = ((stage1, 0), (stage2, 3), (stage3, 8), (stage4, 13), (finish, 18))
-    for t in range(items + 18):
+    stages = ((stage1, 0), (stage2, 4), (stage3, 8), (stage4, 11), (finish, 14))
+    for t in range(items + 14):
         for stage, late in stages:
             if 0 <= t - late < items:
                 stage(t - late)
@@ -553,18 +564,7 @@
             csend[...] = jnp.sum(cbuf[:, 1], axis=0)
             count_back.start()
             number = (lax.broadcasted_iota(jnp.int32, (4, BLOCK), 0) + 1).astype(F32)
-            pieces = []
-            for s in range(16):
-                q, turn = s // 2, 1 - 2 * (s % 2)
-                d = lax.rem(turn * (z - q) + 16, 8)
-                at_home = (d <= 2) | (d == 7)
-                who = jnp.where(at_home, s, lax.rem(q - 3 * turn + 8, 8) * 2 + s % 2)
-                d = jnp.where(at_home, d, lax.rem(d + 3, 8))
-                pos = jnp.where(d == 0, 0, jnp.where(d == 1, 1, jnp.where(d == 7, 2, 3)))
-                row = pos * 2 + jnp.where(at_home, 0, 1)
-                here = ct[s, z, lane_of(0), :] == number
-                pieces.append(jnp.where(here, st[who, row, lane_of(0), :], NEG))
-            lognorm[...] = log_sum(pieces)
+            lognorm[...] = log_sums(0, number, lane_of(0))
         if t == items + 4:
             count_back.wait_recv()
             count = jnp.sum(cbuf[:, 0], axis=0) + cret[...]
@@ -613,10 +613,10 @@
     def sent(d):
         for copy in (code_copy, spread_copy, cnt_copy):
             copy(d).wait_send()
-        for n in range(2):
-            stat_copy(n, d).wait_send()
 
     each(sent)
+    for one in stats(0) + stats(1):
+        stat_copy(*one, False).wait_send()
 
     each(pa_wait)
     peaks[m] = jnp.max(pa[...], axis=0)
@@ -687,7 +687,7 @@
             vmem((16, 8, 2, BLOCK), F32),
             vmem((16, 8, 2, BLOCK), F32),
             vmem((8, 2, BLOCK), F32),
-            vmem((2, 8, 2, BLOCK), F32),
+            vmem((2, 4, 2, BLOCK), F32),
             vmem((2, width, BLOCK), F32),
             vmem((2, width, BLOCK), F32),
             vmem((16, 2, 1, width), F32),

time: 174 us -> 172 us (0.989)
  Pallas kernels: 174 us -> 172 us
    pallas_call x1, Pallas kernels: 172 us -> 170 us  [on_device(): pl.pallas_call(kernel, name='kmeans_step', out_shape=(jax.ShapeDtypeStruc...]
where the time goes in v6:
time: 172 us
  Pallas kernels  172 us (100%)
    pallas_call x1, Pallas kernels, on_device(): pl.pallas_call(kernel, name='kmeans_step', out_shape=(jax.ShapeDtypeStruc...  170 us

profile of v6, /device:TPU:1, one launch (start us, length us, event | category | flops | bytes accessed | tf_op | source)
XLA Modules:
  0.0 172.4 jit_solution(5587131619124256744)
XLA Ops:
  0.6 169.9 %kmeans_step.1 = (f32[48,2048]{1,0:T(8,128)}, f32[1,128]{1,0:T(1,128)}, f32[4,128]{1,0:T(4,128)}, f32[16,1,128]{2,1,0:T(1,128)}) custom-call(bf16[512,2048]{1,0:T(8,128)(2,1)} %data_in.1, bf16[768,2048]{1,0:T(8,128)(2,1)} %cent_in.1, s32[4,16]{1,0:T(4,128)} %bitcast.3), custom_call_target="tpu_custom_call" | custom-call | tf_op jit(solution)/shard_map/kmeans_step/pallas_call | solution.py:654
  170.6 1.8 %outputs.1 = (f32[48,2048]{1,0:T(8,128)}, f32[1,48]{1,0:T(1,128)}, f32[4,128]{1,0:T(4,128)}, f32[16,512]{1,0:T(8,128)}) custom-call(f32[48,2048]{1,0:T(8,128)} %get-tuple-element.12.made, f32[1,128]{1,0:T(1,128)} %get-tuple-element.13.width, f32[4,128]{1,0:T(4,128)} %get-tuple-element.14.logs, f32[16,1,128]{2,1,0:T(1,128)} %get-tuple-element.15.peaks, ...), custom_call_target="tpu_custom_call" | custom-call | tf_op jit(solution)/shard_map/outputs/pallas_call | solution.py:728

commit v7 on v6

--- a/solution.py
+++ b/solution.py
@@ -325,17 +325,17 @@
         scores(1, pos)
 
     early = {0: (0, 6), 1: (0, 6), -1: (0, 6), 2: (0, 4), -2: (2, 6), 3: (0, 2), -3: (4, 6)}
-    final = {k: (6 if k >= 0 else 7, 7 if 0 < k < 4 else 8) for k in range(-3, 5)}
+    groups = (early, {k: (7, 8) for k in (-3, -2, -1, 0, 4)}, {k: (6, 7) for k in range(5)})
     peers = [(k, j) for k in range(-3, 5) for j in range(2) if (k, j) != (0, 0)]
 
     def stat_copy(n, k, j, came):
-        rows = (early, final)[n][k]
+        rows = groups[n][k]
         src = m if not came else at(-k, 0) if j == 0 else at(k, 1)
         ref, i = st.at[src, rows[0] : rows[1]], (k + 3) * 2 + j
         return rcopy(ref, ref, stat_s.at[n, i], stat_r.at[n, i], {"mp": src} if came else dev(k, j))
 
     def stats(n):
-        return [(n, k, j) for k, j in peers if n == 1 or k < 4]
+        return [(n, k, j) for k, j in peers if k in groups[n]]
 
     for one in stats(0):
         stat_copy(*one, False).start()
@@ -350,9 +350,12 @@
                 sc[n * 4 + 3] = prod.reshape(sc.shape[1:])
             else:
                 weigh_up(n, 3, sc[n * 4 + 3].reshape(width, 256) + prod)
-    for one in stats(1):
+                if n == 1:
+                    for one in stats(1):
+                        stat_copy(*one, False).start()
+    for one in stats(2):
         stat_copy(*one, False).start()
-    for one in stats(0) + stats(1):
+    for one in stats(0) + stats(1) + stats(2):
         stat_copy(*one, True).wait_recv()
 
     def log_sum(pieces):
@@ -615,7 +618,7 @@
             copy(d).wait_send()
 
     each(sent)
-    for one in stats(0) + stats(1):
+    for one in stats(0) + stats(1) + stats(2):
         stat_copy(*one, False).wait_send()
 
     each(pa_wait)
@@ -708,8 +711,8 @@
             dma((3, 2, 2)),
             dma((2, 2, 2)),
             dma((2, 2, 2)),
-            dma((2, 16)),
-            dma((2, 16)),
+            dma((3, 16)),
+            dma((3, 16)),
             dma((16,)),
             dma((16,)),
             *[dma((items, 2)) for _ in range(10)],

time: 172 us -> 173 us (level)
  no operation moved by 1% of the time
where the time goes in v7:
time: 173 us; the launch traced here: 172 us
  Pallas kernels  172 us (99%)
    pallas_call x1, Pallas kernels, on_device(): pl.pallas_call(kernel, name='kmeans_step', out_shape=(jax.ShapeDtypeStruc...  170 us

profile of v7, /device:TPU:1, one launch (start us, length us, event | category | flops | bytes accessed | tf_op | source)
XLA Modules:
  0.0 172.4 jit_solution(11454446039385581070)
XLA Ops:
  0.6 170.0 %kmeans_step.1 = (f32[48,2048]{1,0:T(8,128)}, f32[1,128]{1,0:T(1,128)}, f32[4,128]{1,0:T(4,128)}, f32[16,1,128]{2,1,0:T(1,128)}) custom-call(bf16[512,2048]{1,0:T(8,128)(2,1)} %data_in.1, bf16[768,2048]{1,0:T(8,128)(2,1)} %cent_in.1, s32[4,16]{1,0:T(4,128)} %bitcast.3), custom_call_target="tpu_custom_call" | custom-call | tf_op jit(solution)/shard_map/kmeans_step/pallas_call | solution.py:657
  170.6 1.8 %outputs.1 = (f32[48,2048]{1,0:T(8,128)}, f32[1,48]{1,0:T(1,128)}, f32[4,128]{1,0:T(4,128)}, f32[16,512]{1,0:T(8,128)}) custom-call(f32[48,2048]{1,0:T(8,128)} %get-tuple-element.12.made, f32[1,128]{1,0:T(1,128)} %get-tuple-element.13.width, f32[4,128]{1,0:T(4,128)} %get-tuple-element.14.logs, f32[16,1,128]{2,1,0:T(1,128)} %get-tuple-element.15.peaks, ...), custom_call_target="tpu_custom_call" | custom-call | tf_op jit(solution)/shard_map/outputs/pallas_call | solution.py:731
